TPU v7x, 128 devices: a whole 4x4x4 slice. The times are simulated.
128 devices in a mesh: dp: 8 (over y_lo, z), head: 16 (over x, y_hi, core).
Axes of the slice: x: 4, y: 4 (y_hi: 2, y_lo: 2; y = y_hi * 2 + y_lo), z: 4, core: 2. Of those that a mesh axis runs over, the one named last changes fastest.
Arguments:
- projected: bfloat16 [49152, 24576], P(('dp', 'head')), may hold values from -64 to 64, as said below
- weight_exp: int32 [49152], P(('dp', 'head')), may hold values from 0 to 3
- damp_exp: int32 [128], replicated, may hold values from 0 to 2
Outputs:
- whitening: float32 [128, 192, 192], P('head')
Inputs may be any that keep to these rules, and one draw needn't show every extreme that they name: `projected`: real values.
All inputs are finite; a program needn't handle non-finite values.
Results may differ from a plain program's by a relative error of at most 0.0003.
Values may be sent and summed in bfloat16 or wider, within the bound.
A program may use at most 192 MiB of HBM per device.

v0:
```python
import functools

import jax
import jax.numpy as jnp
from jax import lax
from jax.experimental import pallas as pl
from jax.experimental.pallas import tpu as pltpu
from jax.sharding import PartitionSpec as P

HD = 192
BLK = HD // 3
HIGH = lax.Precision.HIGHEST


def store_pair(rows, wide, out, at):
    weighted = rows * wide
    contract = (((0,), (0,)), ((), ()))
    width = 4 * BLK
    first = lax.dot_general(rows[:, :width], weighted[:, :width], contract, preferred_element_type=jnp.float32)
    second = lax.dot_general(rows[:, -width:], weighted[:, -width:], contract, preferred_element_type=jnp.float32)
    two = 2 * BLK
    lanes = lax.broadcasted_iota(jnp.int32, (BLK, two), 1)
    corner = pltpu.roll(first[two : two + BLK, two:], BLK, 1)
    out[at, :BLK, :] = jnp.where(lanes < BLK, first[:BLK, :two], corner)
    out[at, BLK:, :] = first[BLK:HD, :two]
    out[at + 1, :two, :] = second[BLK : BLK + two, two:]
    corner = pltpu.roll(second[BLK:two, :two], BLK, 1)
    out[at + 1, two:, :] = jnp.where(lanes < BLK, corner, second[HD:, two:])


def dot(a, b):
    return lax.dot_general(a, b, (((1,), (0,)), ((), ())), precision=HIGH, preferred_element_type=jnp.float32)


def dot_t(a, b):
    return lax.dot_general(a, b, (((1,), (1,)), ((), ())), precision=HIGH, preferred_element_type=jnp.float32)


def inverse_factors(blocks):
    lane = lax.broadcasted_iota(jnp.int32, (8, BLK), 1)
    sub = lax.broadcasted_iota(jnp.int32, (8, BLK), 0)
    sub1 = lax.broadcasted_iota(jnp.int32, (8, 1), 0)
    groups = BLK // 8
    held = [[block[8 * g : 8 * g + 8] for g in range(groups)] for block in blocks]
    for k in range(BLK):
        own, spot = divmod(k, 8)
        is_k = lane == k
        for parts in held:
            row = parts[own][spot : spot + 1, :]
            scale = 1.0 / row[:, k : k + 1]
            row = jnp.where(is_k[:1], 1.0, row) * scale
            for g in range(own, groups):
                part = parts[g]
                column = part[:, k : k + 1]
                if g == own:
                    if spot == 7:
                        continue
                    column = jnp.where(sub1 > spot, column, 0.0)
                    kept = jnp.where(is_k & (sub > spot), 0.0, part)
                else:
                    kept = jnp.where(is_k, 0.0, part)
                parts[g] = kept - column * row
    out = []
    for parts in held:
        rows = []
        for g in range(groups):
            ids = sub + 8 * g
            pivot = jnp.sum(jnp.where(lane == ids, parts[g], 0.0), axis=1, keepdims=True)
            unit = jnp.where(lane < ids, parts[g], jnp.where(lane == ids, 1.0, 0.0))
            rows.append(unit * (1.0 / jnp.sqrt(pivot)))
        out.append(jnp.concatenate(rows, axis=0))
    return out


def unpack_even(got):
    two = 2 * BLK
    return got[:BLK, :BLK], got[BLK:two, BLK:], got[:BLK, BLK:], got[BLK:, :BLK], got[two:, BLK:]


def unpack_odd(got):
    two = 2 * BLK
    return got[two:, :BLK], got[BLK:two, :BLK], got[two:, BLK:], got[:BLK, :].T, got[BLK:two, BLK:].T


def whiten_kernel(total, count, damp_ref, packed_ref, out_ref):
    two = 2 * BLK
    diag = lax.broadcasted_iota(jnp.int32, (BLK, BLK), 0) == lax.broadcasted_iota(jnp.int32, (BLK, BLK), 1)
    a11, a22, a33, low, a32 = [], [], [], [], []
    for m in range(count):
        got = packed_ref[m] / total
        even = unpack_even(got)
        odd = unpack_odd(got)
        if count % 2 == 0:
            d1, d2, d3, left, corner = odd if m % 2 else even
        else:
            turn = (lax.axis_index("head") * lax.axis_size("dp") + lax.axis_index("dp")) * count + m
            d1, d2, d3, left, corner = (jnp.where(turn % 2 == 0, a, b) for a, b in zip(even, odd))
        trace = jnp.sum(jnp.where(diag, d1 + d2 + d3, 0.0), axis=(0, 1), keepdims=True)
        level = trace / HD + 1e-06
        shift = jnp.where(diag, damp_ref[m] * level, 0.0)
        a11.append(d1 + shift)
        a22.append(d2 + shift)
        a33.append(d3 + shift)
        low.append(left)
        a32.append(corner)
    each = range(count)
    w11 = inverse_factors(a11)
    l1 = [dot_t(low[m], w11[m]) for m in each]
    square = [dot_t(l1[m], l1[m]) for m in each]
    w22 = inverse_factors([a22[m] - square[m][:BLK, :BLK] for m in each])
    l32 = [dot_t(a32[m] - square[m][BLK:, :BLK], w22[m]) for m in each]
    w33 = inverse_factors([a33[m] - square[m][BLK:, BLK:] - dot_t(l32[m], l32[m]) for m in each])
    for m in each:
        below = dot(l1[m], w11[m])
        w21 = -dot(w22[m], below[:BLK])
        w32 = -dot(w33[m], dot(l32[m], w22[m]))
        w31 = -dot(w33[m], below[BLK:] + dot(l32[m], w21))
        out_ref[m, :BLK] = jnp.concatenate((w11[m], w33[m]), axis=1)
        out_ref[m, BLK:two] = jnp.concatenate((w21, w22[m]), axis=1)
        out_ref[m, two:] = jnp.concatenate((w31, w32), axis=1)


def whiten(packed, damp, total):
    count = packed.shape[0]
    return pl.pallas_call(
        functools.partial(whiten_kernel, total, count),
        in_specs=[pl.BlockSpec(memory_space=pltpu.SMEM), pl.BlockSpec(memory_space=pltpu.VMEM)],
        out_specs=pl.BlockSpec(memory_space=pltpu.VMEM),
        out_shape=jax.ShapeDtypeStruct(packed.shape, jnp.float32),
    )(damp, packed)


def flip(index, step):
    return index + step * (1 - 2 * ((index // step) % 2))


def remote(src, dst, sems, slot, device):
    return pltpu.make_async_remote_copy(
        src_ref=src,
        dst_ref=dst,
        send_sem=sems.at[0, slot],
        recv_sem=sems.at[1, slot],
        device_id=device,
        device_id_type=pl.DeviceIdType.MESH,
    )


def greet(heads, dps):
    barrier = pltpu.get_barrier_semaphore()
    for peer in heads:
        pl.semaphore_signal(barrier, inc=1, device_id={"head": peer}, device_id_type=pl.DeviceIdType.MESH)
    for peer in dps:
        pl.semaphore_signal(barrier, inc=1, device_id={"dp": peer}, device_id_type=pl.DeviceIdType.MESH)
    pl.semaphore_wait(barrier, len(heads) + len(dps))


def part_rows():
    last = HD // 4
    first = (HD - last) // 2
    return (0, first), (first, first), (2 * first, last)


def scatter_kernel(n_head, n_dp, share, rows_ref, weights_ref, out_ref, acc, sent, own_grams, wide, columns, got_a, got_b, got_c, got_z, got_y, sem_in, sem_0, sem_a, sem_b, sem_c, sem_z, sem_y):
    head = lax.axis_index("head")
    dp = lax.axis_index("dp")
    chunks = n_head // 2
    bits = chunks.bit_length() - 1
    mine = head // 2
    core = head % 2
    per_head = share * n_dp
    span = per_head * HD
    peers = [lax.rem(dp + o, n_dp) for o in range(1, n_dp)]
    part_a, part_b, part_c = part_rows()
    up = list(range(bits))
    down = up[::-1]
    rows_c = pl.ds(part_c[0], part_c[1])

    def chunk_of(e):
        chunk = mine
        for j in range(bits):
            if (e >> j) & 1:
                chunk = chunk + (1 - 2 * ((mine // (1 << j)) % 2)) * (1 << j)
        return chunk

    order = list(range(chunks))[::-1]
    visits = []
    for e in order:
        visits += [2 * chunk_of(e) + 1 - core, 2 * chunk_of(e) + core]

    def fetch(v):
        start = pl.multiple_of(visits[v] * span, 2 * BLK)
        return pltpu.make_async_copy(rows_ref.at[:, pl.ds(start, span)], columns.at[v % 2], sem_in.at[v % 2])

    fetch(0).start()
    wide[...] = jnp.broadcast_to(weights_ref[...], wide.shape)
    greet([flip(head, 1 << j) for j in range(bits + 1)], peers)

    def multiply(v, out):
        if v + 1 < len(visits):
            fetch(v + 1).start()
        fetch(v).wait()

        def pair(i, carry):
            start = pl.multiple_of(i * 2 * HD, 2 * BLK)
            store_pair(columns[v % 2, :, pl.ds(start, 2 * HD)], wide[...], out, 2 * i)
            return carry

        lax.fori_loop(0, per_head // 2, pair, 0, unroll=2)

    def squeeze(e, j):
        return (e >> (j + 1) << j) | (e & ((1 << j) - 1))

    early = {"a": [], "b": []}
    flight_z = []
    for n, e in enumerate(order):
        c = chunk_of(e)
        multiply(2 * n, sent.at[n])
        copy = remote(sent.at[n], acc.at[c], sem_0, n, {"head": flip(head, 1)})
        copy.start()
        multiply(2 * n + 1, own_grams)
        copy.wait()

        def add(m, carry, c=c):
            acc[c, m] += own_grams[m]
            return carry

        lax.fori_loop(0, per_head, add, 0)
        for name, (start, size), got, sems, j in (("a", part_a, got_a, sem_a, up[0]), ("b", part_b, got_b, sem_b, down[0])):
            if (e >> j) & 1:
                slot = squeeze(e, j)
                out = remote(
                    acc.at[c, pl.ds(0, per_head), pl.ds(start, size)], got.at[slot], sems, slot, {"head": flip(head, 2 << j)}
                )
                out.start()
                early[name].append((out, chunk_of(e ^ (1 << j)), slot))
        for o, peer in enumerate(peers):
            out = remote(
                acc.at[c, pl.ds(peer * share, share), rows_c], got_z.at[o, e], sem_z, o * chunks + e, {"dp": peer}
            )
            out.start()
            flight_z.append(out)

    def begin(part, got, sems, order, step, first, count):
        j = order[step]
        bit = (mine // (1 << j)) % 2
        fixed = 0
        for done in order[:step]:
            fixed = fixed + (mine // (1 << done)) % 2 * (1 << done)
        free = [b for b in range(bits) if b not in order[: step + 1]]
        flight = []
        start, size = part
        offset = sum(chunks >> (s + 1) for s in range(step))
        for e in range(1 << len(free)):
            base = fixed + sum(((e >> i) & 1) << b for i, b in enumerate(free))
            slot = offset + e
            copy = remote(
                acc.at[base + (1 - bit) * (1 << j), pl.ds(first, count), pl.ds(start, size)],
                got.at[slot],
                sems,
                slot,
                {"head": flip(head, 2 << j)},
            )
            copy.start()
            flight.append((copy, base + bit * (1 << j), slot))
        return flight, part, got, first, count

    def finish(state):
        flight, (start, size), got, first, count = state
        for copy, keep, slot in flight:
            copy.wait()

            def add(m, carry, keep=keep, slot=slot):
                acc[keep, first + m, start : start + size] += got[slot, m]
                return carry

            lax.fori_loop(0, count, add, 0)

    own = dp * share
    for step in range(bits):
        if step:
            state_a = begin(part_a, got_a, sem_a, up, step, 0, per_head)
            state_b = begin(part_b, got_b, sem_b, down, step, 0, per_head)
        else:
            state_a = early["a"], part_a, got_a, 0, per_head
            state_b = early["b"], part_b, got_b, 0, per_head
        finish(state_a)
        finish(state_b)
    rows_ab = pl.ds(0, part_c[0])
    flight_y = []
    for o, peer in enumerate(peers):
        copy = remote(acc.at[mine, pl.ds(peer * share, share), rows_ab], got_y.at[o], sem_y, o, {"dp": peer})
        copy.start()
        flight_y.append(copy)
    for copy in flight_z:
        copy.wait()
    for e in range(chunks):

        def add_z(m, carry, c=chunk_of(e), e=e):
            value = acc[c, own + m, part_c[0] :]
            for o in range(len(peers)):
                value += got_z[o, e, m]
            acc[c, own + m, part_c[0] :] = value
            return carry

        lax.fori_loop(0, share, add_z, 0)
    for step in range(bits):
        finish(begin(part_c, got_c, sem_c, up, step, own, share))
    for copy in flight_y:
        copy.wait()

    def add_y(m, carry):
        value = acc[mine, own + m, : part_c[0]]
        for o in range(len(peers)):
            value += got_y[o, m]
        out_ref[m, : part_c[0]] = value
        out_ref[m, part_c[0] :] = acc[mine, own + m, part_c[0] :]
        return carry

    lax.fori_loop(0, share, add_y, 0)


def gram_sums(projected, weights, n_head, n_dp):
    tokens, width = projected.shape
    mats, rows, lanes = width // HD, HD, 2 * BLK
    per_head = mats // n_head
    share = per_head // n_dp
    chunks = n_head // 2
    (_, rows_a), (_, rows_b), (_, rows_c) = part_rows()
    f32 = jnp.float32
    return pl.pallas_call(
        functools.partial(scatter_kernel, n_head, n_dp, share),
        in_specs=[pl.BlockSpec(memory_space=pl.ANY), pl.BlockSpec(memory_space=pltpu.VMEM)],
        out_specs=pl.BlockSpec(memory_space=pltpu.VMEM),
        out_shape=jax.ShapeDtypeStruct((share, rows, lanes), f32),
        scratch_shapes=[
            pltpu.VMEM((chunks, per_head, rows, lanes), f32),
            pltpu.VMEM((chunks, per_head, rows, lanes), f32),
            pltpu.VMEM((per_head, rows, lanes), f32),
            pltpu.VMEM((tokens, 2 * HD), projected.dtype),
            pltpu.VMEM((2, tokens, per_head * HD), projected.dtype),
            pltpu.VMEM((chunks - 1, per_head, rows_a, lanes), f32),
            pltpu.VMEM((chunks - 1, per_head, rows_b, lanes), f32),
            pltpu.VMEM((chunks - 1, share, rows_c, lanes), f32),
            pltpu.VMEM((n_dp - 1, chunks, share, rows_c, lanes), f32),
            pltpu.VMEM((n_dp - 1, share, rows - rows_c, lanes), f32),
            pltpu.SemaphoreType.DMA((2,)),
            pltpu.SemaphoreType.DMA((2, chunks)),
            pltpu.SemaphoreType.DMA((2, chunks - 1)),
            pltpu.SemaphoreType.DMA((2, chunks - 1)),
            pltpu.SemaphoreType.DMA((2, chunks - 1)),
            pltpu.SemaphoreType.DMA((2, (n_dp - 1) * chunks)),
            pltpu.SemaphoreType.DMA((2, n_dp - 1)),
        ],
        compiler_params=pltpu.CompilerParams(collective_id=0, has_side_effects=True, vmem_limit_bytes=60 << 20),
    )(projected, weights)


def gather_kernel(n_dp, share, packed_ref, out_ref, got, sems):
    dp = lax.axis_index("dp")
    peers = [lax.rem(dp + o, n_dp) for o in range(1, n_dp)]
    greet([], peers)
    flight = []
    for o, peer in enumerate(peers):
        copy = remote(packed_ref, got.at[o], sems, o, {"dp": peer})
        copy.start()
        flight.append(copy)
    two = 2 * BLK

    def unpack(source, base):
        def one(m, carry):
            top = source[m, :BLK]
            out_ref[base + m, :BLK, :two] = jnp.where(lax.broadcasted_iota(jnp.int32, (BLK, two), 1) < BLK, top, 0.0)
            out_ref[base + m, BLK:, :two] = source[m, BLK:]
            out_ref[base + m, :two, two:] = jnp.zeros((two, BLK), jnp.float32)
            out_ref[base + m, two:, two:] = top[:, BLK:]
            return carry

        lax.fori_loop(0, share, one, 0)

    unpack(packed_ref, dp * share)
    for o in range(n_dp - 1):
        flight[o].wait()
        unpack(got.at[o], lax.rem(dp + n_dp - 1 - o, n_dp) * share)


def gather(packed, n_dp):
    share, rows, lanes = packed.shape
    return pl.pallas_call(
        functools.partial(gather_kernel, n_dp, share),
        in_specs=[pl.BlockSpec(memory_space=pltpu.VMEM)],
        out_specs=pl.BlockSpec(memory_space=pltpu.VMEM),
        out_shape=jax.ShapeDtypeStruct((n_dp * share, HD, HD), jnp.float32),
        scratch_shapes=[
            pltpu.VMEM((n_dp - 1, share, rows, lanes), jnp.float32),
            pltpu.SemaphoreType.DMA((2, n_dp - 1)),
        ],
        compiler_params=pltpu.CompilerParams(collective_id=1, has_side_effects=True),
    )(packed)


def on_device(projected, weight_exp, damp_exp):
    n_head = lax.axis_size("head")
    n_dp = lax.axis_size("dp")
    mats = projected.shape[1] // HD
    share = mats // (n_head * n_dp)
    total = projected.shape[0] * n_head * n_dp
    weights = jnp.exp2(weight_exp.astype(jnp.float32)).astype(jnp.bfloat16)
    owned = gram_sums(projected, weights[:, None], n_head, n_dp)
    first = (lax.axis_index("head") * n_dp + lax.axis_index("dp")) * share
    damp = jnp.exp2(-lax.dynamic_slice_in_dim(damp_exp, first, share, 0).astype(jnp.float32))
    factors = whiten(owned, damp, float(total))
    return gather(factors, n_dp)


def solution(mesh):
    return jax.shard_map(
        on_device,
        mesh=mesh,
        in_specs=(P(("dp", "head"), None), P(("dp", "head")), P()),
        out_specs=P("head", None, None),
        check_vma=False,
    )
```

profile of v0, /device:TPU:0, one launch (start us, length us, event | category | flops | bytes accessed | tf_op | source)
XLA Modules:
  0.0 143.4 jit_solution(7450352635504376729)
XLA Ops:
  0.0 1.2 dynamic_slice.3
  1.9 0.7 exponential_convert_fusion
  2.6 0.8 broadcast_in_dim.4.weights_ref
  3.4 106.3 %shard_map.37.packed_ref = f32[1,192,128]{2,1,0:T(8,128)} custom-call(bf16[384,24576]{1,0:T(8,128)(2,1)} %rows_ref.1, bf16[384,1]{1,0:T(8,128)(2,1)} %broadcast_in_dim.4.weights_ref), custom_call_target="tpu_custom_call" | custom-call | tf_op jit(solution)/shard_map/pallas_call | solution.py:330
  109.7 19.2 %shard_map.38.packed_ref = f32[1,192,128]{2,1,0:T(8,128)} custom-call(f32[1]{0:T(128)S(6)} %exp2.16.damp_ref, f32[1,192,128]{2,1,0:T(8,128)} %shard_map.37.packed_ref), custom_call_target="tpu_custom_call" | custom-call | tf_op jit(solution)/shard_map/pallas_call | solution.py:125
  129.0 11.7 %shard_map.39 = f32[8,192,192]{2,1,0:T(8,128)} custom-call(f32[1,192,128]{2,1,0:T(8,128)} %shard_map.38.packed_ref), custom_call_target="tpu_custom_call" | custom-call | tf_op jit(solution)/shard_map/pallas_call | solution.py:388
  140.7 2.7 %copy.6 = f32[8,192,192]{2,1,0:T(8,128)} copy(f32[8,192,192]{2,1,0:T(8,128)} %shard_map.39) | data formatting | bytes 2359296
where the time goes:
time: 144 us; the launch traced here: 143 us
  Pallas kernels  137 us (95%)
  local copies, waits for them, and re-layouts  4.66 us (3%)
    pallas_call x1, Pallas kernels, gram_sums(): pl.pallas_call(functools.partial(scatter_kernel, n_head, n_dp, share), in...  106 us
    pallas_call x1, Pallas kernels, whiten(): pl.pallas_call(functools.partial(whiten_kernel, total, count), in_specs=[...  19.2 us
    pallas_call x1, Pallas kernels, gather(): pl.pallas_call(functools.partial(gather_kernel, n_dp, share), in_specs=[p...  11.7 us

commit v1 on v0

v1 whole, which is shorter than its diff:
```python
import functools

import jax
import jax.numpy as jnp
from jax import lax
from jax.experimental import pallas as pl
from jax.experimental.pallas import tpu as pltpu
from jax.sharding import PartitionSpec as P

HD = 192
BLK = HD // 3
HIGH = lax.Precision.HIGHEST


def store_pair(rows, wide, out, at, after):
    weighted = rows * wide
    contract = (((0,), (0,)), ((), ()))
    width = 4 * BLK
    first = lax.dot_general(rows[:, :width], weighted[:, :width], contract, preferred_element_type=jnp.float32)
    second = lax.dot_general(rows[:, -width:], weighted[:, -width:], contract, preferred_element_type=jnp.float32)
    two = 2 * BLK
    lanes = lax.broadcasted_iota(jnp.int32, (BLK, two), 1)
    corner = pltpu.roll(first[two : two + BLK, two:], BLK, 1)
    out[at, :BLK, :] = jnp.where(lanes < BLK, first[:BLK, :two], corner)
    out[at, BLK:, :] = first[BLK:HD, :two]
    out[after, :two, :] = second[BLK : BLK + two, two:]
    corner = pltpu.roll(second[BLK:two, :two], BLK, 1)
    out[after, two:, :] = jnp.where(lanes < BLK, corner, second[HD:, two:])


def dot(a, b):
    return lax.dot_general(a, b, (((1,), (0,)), ((), ())), precision=HIGH, preferred_element_type=jnp.float32)


def dot_t(a, b):
    return lax.dot_general(a, b, (((1,), (1,)), ((), ())), precision=HIGH, preferred_element_type=jnp.float32)


def inverse_factors(blocks):
    lane = lax.broadcasted_iota(jnp.int32, (8, BLK), 1)
    sub = lax.broadcasted_iota(jnp.int32, (8, BLK), 0)
    sub1 = lax.broadcasted_iota(jnp.int32, (8, 1), 0)
    groups = BLK // 8
    held = [[block[8 * g : 8 * g + 8] for g in range(groups)] for block in blocks]
    for k in range(BLK):
        own, spot = divmod(k, 8)
        is_k = lane == k
        for parts in held:
            row = parts[own][spot : spot + 1, :]
            scale = 1.0 / row[:, k : k + 1]
            row = jnp.where(is_k[:1], 1.0, row) * scale
            for g in range(own, groups):
                part = parts[g]
                column = part[:, k : k + 1]
                if g == own:
                    if spot == 7:
                        continue
                    column = jnp.where(sub1 > spot, column, 0.0)
                    kept = jnp.where(is_k & (sub > spot), 0.0, part)
                else:
                    kept = jnp.where(is_k, 0.0, part)
                parts[g] = kept - column * row
    out = []
    for parts in held:
        rows = []
        for g in range(groups):
            ids = sub + 8 * g
            pivot = jnp.sum(jnp.where(lane == ids, parts[g], 0.0), axis=1, keepdims=True)
            unit = jnp.where(lane < ids, parts[g], jnp.where(lane == ids, 1.0, 0.0))
            rows.append(unit * (1.0 / jnp.sqrt(pivot)))
        out.append(jnp.concatenate(rows, axis=0))
    return out


def unpack_even(got):
    two = 2 * BLK
    return got[:BLK, :BLK], got[BLK:two, BLK:], got[:BLK, BLK:], got[BLK:, :BLK], got[two:, BLK:]


def unpack_odd(got):
    two = 2 * BLK
    return got[two:, :BLK], got[BLK:two, :BLK], got[two:, BLK:], got[:BLK, :].T, got[BLK:two, BLK:].T


def whiten_kernel(total, count, damp_ref, packed_ref, out_ref):
    two = 2 * BLK
    diag = lax.broadcasted_iota(jnp.int32, (BLK, BLK), 0) == lax.broadcasted_iota(jnp.int32, (BLK, BLK), 1)
    a11, a22, a33, low, a32 = [], [], [], [], []
    for m in range(count):
        got = packed_ref[m] / total
        even = unpack_even(got)
        odd = unpack_odd(got)
        if count % 2 == 0:
            d1, d2, d3, left, corner = odd if m % 2 else even
        else:
            turn = (lax.axis_index("head") * lax.axis_size("dp") + lax.axis_index("dp")) * count + m
            d1, d2, d3, left, corner = (jnp.where(turn % 2 == 0, a, b) for a, b in zip(even, odd))
        trace = jnp.sum(jnp.where(diag, d1 + d2 + d3, 0.0), axis=(0, 1), keepdims=True)
        level = trace / HD + 1e-06
        shift = jnp.where(diag, damp_ref[m] * level, 0.0)
        a11.append(d1 + shift)
        a22.append(d2 + shift)
        a33.append(d3 + shift)
        low.append(left)
        a32.append(corner)
    each = range(count)
    w11 = inverse_factors(a11)
    l1 = [dot_t(low[m], w11[m]) for m in each]
    square = [dot_t(l1[m], l1[m]) for m in each]
    w22 = inverse_factors([a22[m] - square[m][:BLK, :BLK] for m in each])
    l32 = [dot_t(a32[m] - square[m][BLK:, :BLK], w22[m]) for m in each]
    w33 = inverse_factors([a33[m] - square[m][BLK:, BLK:] - dot_t(l32[m], l32[m]) for m in each])
    for m in each:
        below = dot(l1[m], w11[m])
        w21 = -dot(w22[m], below[:BLK])
        w32 = -dot(w33[m], dot(l32[m], w22[m]))
        w31 = -dot(w33[m], below[BLK:] + dot(l32[m], w21))
        out_ref[m, :BLK] = jnp.concatenate((w11[m], w33[m]), axis=1)
        out_ref[m, BLK:two] = jnp.concatenate((w21, w22[m]), axis=1)
        out_ref[m, two:] = jnp.concatenate((w31, w32), axis=1)


def whiten(packed, damp, total):
    count = packed.shape[0]
    return pl.pallas_call(
        functools.partial(whiten_kernel, total, count),
        in_specs=[pl.BlockSpec(memory_space=pltpu.SMEM), pl.BlockSpec(memory_space=pltpu.VMEM)],
        out_specs=pl.BlockSpec(memory_space=pltpu.VMEM),
        out_shape=jax.ShapeDtypeStruct(packed.shape, jnp.float32),
    )(damp, packed)


def remote(src, dst, send, recv, device):
    return pltpu.make_async_remote_copy(
        src_ref=src, dst_ref=dst, send_sem=send, recv_sem=recv, device_id=device, device_id_type=pl.DeviceIdType.MESH
    )


def greet(devices):
    barrier = pltpu.get_barrier_semaphore()
    for device in devices:
        pl.semaphore_signal(barrier, inc=1, device_id=device, device_id_type=pl.DeviceIdType.MESH)
    pl.semaphore_wait(barrier, len(devices))


RING = 4
HALF = BLK // 2
FAR_FIRST = (2, 1, 3, 0)
ORDERS = ((0, 1, 2), (1, 2, 0), (2, 0, 1))
AHEAD = 2
VISITS = sorted(
    ((a, b) for a in range(RING) for b in range(RING)),
    key=lambda s: ((s[0] != 2) + (s[1] != 2), (s[0] == 0) + (s[1] == 0)),
)


def place():
    head = lax.axis_index("head")
    dp = lax.axis_index("dp")
    return head // 4, head // 2 % 2 * 2 + dp // RING, dp % RING, head % 2


def neighbour(axis, step):
    spot = list(place())
    spot[axis] = (spot[axis] + step) % RING
    x, y, z, core = spot
    return {"head": (x * 2 + y // 2) * 2 + core, "dp": y % 2 * RING + z}


class Stage:
    def __init__(self, part, level, acc, far, near, sem_far, sem_near, sem_send):
        self.part, self.level, self.acc, self.far, self.near = part, level, acc, far, near
        self.sem_far, self.sem_near, self.sem_send = sem_far, sem_near, sem_send
        self.axis = ORDERS[part][level]
        self.free = ORDERS[part][level + 1 :]
        self.to = [neighbour(self.axis, 1), neighbour(self.axis, -1)]

    def pick(self, block, sub):
        spot = [sub.get(a, pl.ds(0, RING)) if a in self.free else pl.ds(0, 1) for a in range(3)]
        spot[self.axis] = pl.ds(block, 1)
        return tuple(spot)

    def rows(self, half):
        return (pl.ds(self.part * BLK + half * HALF, HALF),)

    def far_copy(self, d, sub):
        return remote(
            self.acc.at[self.pick(2, sub) + self.rows(d)],
            self.far.at[(d,) + self.pick(0, sub)],
            self.sem_send.at[0, d],
            self.sem_far.at[d],
            self.to[d],
        )

    def direct_copy(self, d, sub):
        return remote(
            self.acc.at[self.pick((1, 3)[d], sub) + self.rows(1 - d)],
            self.near.at[(d,) + self.pick(0, sub) + (pl.ds((1 - d) * HALF, HALF),)],
            self.sem_send.at[1, d],
            self.sem_near.at[d, RING],
            self.to[d],
        )

    def near_copy(self, d, sub, group):
        return remote(
            self.acc.at[self.pick((1, 3)[d], sub) + self.rows(d)],
            self.near.at[(d,) + self.pick(0, sub) + (pl.ds(d * HALF, HALF),)],
            self.sem_send.at[2, d],
            self.sem_near.at[d, group],
            self.to[d],
        )

    def groups(self):
        if not self.free:
            return [(0, {})]
        return [(g, {self.free[0]: pl.ds(g, 1)}) for g in FAR_FIRST]

    def relay(self, d, group, sub):
        mine = self.pick((1, 3)[d], sub) + self.rows(d)
        self.acc[mine] += self.far[(d,) + self.pick(0, sub)]
        self.near_copy(d, sub, group).start()

    def settle(self, group, sub):
        for d in (0, 1):
            self.near_copy(d, sub, group).wait_recv()
        mine = self.pick(0, sub)
        size = [RING if len(self.free) > 1 and a == self.free[1] else 1 for a in range(3)]
        for i in range(max(size)):
            part = list(mine)
            if len(self.free) > 1:
                part[self.free[1]] = pl.ds(i, 1)
            part = tuple(part)
            rows = (pl.ds(self.part * BLK, BLK),)
            self.acc[part + rows] += self.near[(0,) + part] + self.near[(1,) + part]

    def finish(self):
        for d in (0, 1):
            self.far_copy(d, {}).wait_send()
            self.direct_copy(d, {}).wait_send()
            self.near_copy(d, {}, 0).wait_send()


def stage_shapes(level, part):
    free = ORDERS[part][level + 1 :]
    return tuple(RING if a in free else 1 for a in range(3))


def scatter_kernel(rows_ref, weights_ref, out_ref, acc, sent, got, wide, columns, *rest):
    x, y, z, core = place()
    sem_in, sem_core = rest[-2:]
    stages = [[Stage(part, level, acc, *rest[5 * (3 * level + part) :][:5]) for part in range(3)] for level in range(3)]
    span = RING * HD
    partner = {"head": lax.axis_index("head") // 2 * 2 + 1 - core}
    count = len(VISITS)
    trips = [(0, 0)]
    for i in range(count):
        trips += [(i + 1, 0)] * (i + 1 < count) + [(i, 1)]

    def fetch(v):
        i, own = trips[v]
        to_x, to_y = (x + VISITS[i][0]) % RING, (y + VISITS[i][1]) % RING
        to_core = core if own else 1 - core
        first = ((to_x * 2 + to_y // 2) * 2 + to_core) * 8 + to_y % 2 * RING
        start = pl.multiple_of(first * HD, 2 * BLK)
        slot = v % (AHEAD + 1)
        return pltpu.make_async_copy(rows_ref.at[:, pl.ds(start, span)], columns.at[slot], sem_in.at[slot])

    for v in range(AHEAD):
        fetch(v).start()
    wide[...] = jnp.broadcast_to(weights_ref[...], wide.shape)

    def multiply(v, out):
        if v + AHEAD < len(trips):
            fetch(v + AHEAD).start()
        fetch(v).wait()

        def pair(i, carry):
            start = pl.multiple_of(i * 2 * HD, 2 * BLK)
            even = (2 * i + RING - z) % RING
            store_pair(columns[v % (AHEAD + 1), :, pl.ds(start, 2 * HD)], wide[...], out, even, (even + 1) % RING)
            return carry

        lax.fori_loop(0, RING // 2, pair, 0, unroll=True)

    def exchange(i):
        return remote(sent.at[i], got.at[i], sem_core.at[0, i], sem_core.at[1, i], partner)

    def release(i):
        a, b = VISITS[i]
        exchange(i).wait_recv()

        def add(m, carry):
            acc[a, b, m] += got[i, m]
            return carry

        lax.fori_loop(0, RING, add, 0)
        spots = ({1: pl.ds(b, 1)}, {0: pl.ds(a, 1)}, {0: pl.ds(a, 1), 1: pl.ds(b, 1)})
        for stage, at, sub in zip(stages[0], (a, b, None), spots):
            for d in (0, 1):
                if at in (2, None):
                    stage.far_copy(d, sub).start()
            for d in (0, 1):
                if at in ((1, 3)[d], None):
                    stage.direct_copy(d, sub).start()

    for v, (i, own) in enumerate(trips):
        if own:
            multiply(v, acc.at[VISITS[i]])
            if i:
                release(i - 1)
        else:
            multiply(v, sent.at[i])
            if v == 0:
                greet([partner] + [to for stage in stages[0] for to in stage.to])
            exchange(i).start()
    release(count - 1)
    for level in range(3):
        now = stages[level]
        for stage in now:
            for d in (0, 1):
                stage.far_copy(d, {}).wait_recv()
                for group, sub in stage.groups():
                    stage.relay(d, group, sub)
        for stage in now:
            for d in (0, 1):
                stage.direct_copy(d, {}).wait_recv()
        for n in range(len(now[0].groups())):
            for part in range(3):
                group, sub = now[part].groups()[n]
                now[part].settle(group, sub)
                if level < 2:
                    later = stages[level + 1][part]
                    if group == 2:
                        later.far_copy(0, {}).start()
                        later.far_copy(1, {}).start()
                    elif group:
                        later.direct_copy(group // 2, {}).start()
    out_ref[0] = acc[0, 0, 0]
    for i in range(count):
        exchange(i).wait_send()
    for level in stages:
        for stage in level:
            stage.finish()


def gram_sums(projected, weights):
    tokens, width = projected.shape
    rows, lanes = HD, 2 * BLK
    f32 = jnp.float32
    rings = []
    for level in range(3):
        for part in range(3):
            shape = stage_shapes(level, part)
            rings += [
                pltpu.VMEM((2,) + shape + (HALF, lanes), f32),
                pltpu.VMEM((2,) + shape + (BLK, lanes), f32),
                pltpu.SemaphoreType.DMA((2,)),
                pltpu.SemaphoreType.DMA((2, RING + 1)),
                pltpu.SemaphoreType.DMA((3, 2)),
            ]
    return pl.pallas_call(
        scatter_kernel,
        in_specs=[pl.BlockSpec(memory_space=pl.ANY), pl.BlockSpec(memory_space=pltpu.VMEM)],
        out_specs=pl.BlockSpec(memory_space=pltpu.VMEM),
        out_shape=jax.ShapeDtypeStruct((1, rows, lanes), f32),
        scratch_shapes=[
            pltpu.VMEM((RING, RING, RING, rows, lanes), f32),
            pltpu.VMEM((len(VISITS), RING, rows, lanes), f32),
            pltpu.VMEM((len(VISITS), RING, rows, lanes), f32),
            pltpu.VMEM((tokens, 2 * HD), projected.dtype),
            pltpu.VMEM((AHEAD + 1, tokens, RING * HD), projected.dtype),
            *rings,
            pltpu.SemaphoreType.DMA((AHEAD + 1,)),
            pltpu.SemaphoreType.DMA((2, len(VISITS))),
        ],
        compiler_params=pltpu.CompilerParams(collective_id=0, has_side_effects=True, vmem_limit_bytes=60 << 20),
    )(projected, weights)


def gather_kernel(n_dp, share, packed_ref, out_ref, got, sems):
    dp = lax.axis_index("dp")
    peers = [lax.rem(dp + o, n_dp) for o in range(1, n_dp)]
    greet([{"dp": peer} for peer in peers])
    flight = []
    for o, peer in enumerate(peers):
        copy = remote(packed_ref, got.at[o], sems.at[0, o], sems.at[1, o], {"dp": peer})
        copy.start()
        flight.append(copy)
    two = 2 * BLK

    def unpack(source, base):
        def one(m, carry):
            top = source[m, :BLK]
            out_ref[base + m, :BLK, :two] = jnp.where(lax.broadcasted_iota(jnp.int32, (BLK, two), 1) < BLK, top, 0.0)
            out_ref[base + m, BLK:, :two] = source[m, BLK:]
            out_ref[base + m, :two, two:] = jnp.zeros((two, BLK), jnp.float32)
            out_ref[base + m, two:, two:] = top[:, BLK:]
            return carry

        lax.fori_loop(0, share, one, 0)

    unpack(packed_ref, dp * share)
    for o in range(n_dp - 1):
        flight[o].wait()
        unpack(got.at[o], lax.rem(dp + n_dp - 1 - o, n_dp) * share)


def gather(packed, n_dp):
    share, rows, lanes = packed.shape
    return pl.pallas_call(
        functools.partial(gather_kernel, n_dp, share),
        in_specs=[pl.BlockSpec(memory_space=pltpu.VMEM)],
        out_specs=pl.BlockSpec(memory_space=pltpu.VMEM),
        out_shape=jax.ShapeDtypeStruct((n_dp * share, HD, HD), jnp.float32),
        scratch_shapes=[
            pltpu.VMEM((n_dp - 1, share, rows, lanes), jnp.float32),
            pltpu.SemaphoreType.DMA((2, n_dp - 1)),
        ],
        compiler_params=pltpu.CompilerParams(collective_id=1, has_side_effects=True),
    )(packed)


def on_device(projected, weight_exp, damp_exp):
    n_head = lax.axis_size("head")
    n_dp = lax.axis_size("dp")
    mats = projected.shape[1] // HD
    share = mats // (n_head * n_dp)
    total = projected.shape[0] * n_head * n_dp
    weights = jnp.exp2(weight_exp.astype(jnp.float32)).astype(jnp.bfloat16)
    owned = gram_sums(projected, weights[:, None])
    first = (lax.axis_index("head") * n_dp + lax.axis_index("dp")) * share
    damp = jnp.exp2(-lax.dynamic_slice_in_dim(damp_exp, first, share, 0).astype(jnp.float32))
    factors = whiten(owned, damp, float(total))
    return gather(factors, n_dp)


def solution(mesh):
    return jax.shard_map(
        on_device,
        mesh=mesh,
        in_specs=(P(("dp", "head"), None), P(("dp", "head")), P()),
        out_specs=P("head", None, None),
        check_vma=False,
    )
```

time: 144 us -> 90.1 us (0.63)
  Pallas kernels: 137 us -> 83.5 us
    pallas_call x1, Pallas kernels: 106 us -> 51.8 us  [gram_sums(): pl.pallas_call(scatter_kernel, in_specs=[pl.BlockSpec(memory_space=pl.ANY...]
where the time goes in v1:
time: 90.1 us; the launch traced here: 89.6 us
  Pallas kernels  83.5 us (93%)
  local copies, waits for them, and re-layouts  4.66 us (5%)
    pallas_call x1, Pallas kernels, gram_sums(): pl.pallas_call(scatter_kernel, in_specs=[pl.BlockSpec(memory_space=pl.ANY...  51.8 us
    pallas_call x1, Pallas kernels, whiten(): pl.pallas_call(functools.partial(whiten_kernel, total, count), in_specs=[...  19.2 us
    pallas_call x1, Pallas kernels, gather(): pl.pallas_call(functools.partial(gather_kernel, n_dp, share), in_specs=[p...  12.5 us
    unnamed x1, local copies, waits for them, and re-layouts  2.65 us

profile of v1, /device:TPU:0, one launch (start us, length us, event | category | flops | bytes accessed | tf_op | source)
XLA Modules:
  0.0 89.6 jit_solution(11092188150629559770)
XLA Ops:
  0.0 1.2 %dynamic_slice.3 = s32[1]{0:T(128)} dynamic-slice(s32[128]{0:T(128)} %param.5, s32[]{:T(128)S(6)} %select_n.3), dynamic_slice_sizes={1} | dynamic-slice | bytes 12 | tf_op jit(solution)/shard_map/dynamic_slice | solution.py:432
  1.9 0.7 exponential_convert_fusion
  2.6 0.8 broadcast_in_dim.4.weights_ref
  3.4 51.8 %shard_map.37.packed_ref = f32[1,192,128]{2,1,0:T(8,128)} custom-call(bf16[384,24576]{1,0:T(8,128)(2,1)} %rows_ref.1, bf16[384,1]{1,0:T(8,128)(2,1)} %broadcast_in_dim.4.weights_ref), custom_call_target="tpu_custom_call" | custom-call | tf_op jit(solution)/shard_map/pallas_call | solution.py:361
  55.2 19.2 %shard_map.38.packed_ref = f32[1,192,128]{2,1,0:T(8,128)} custom-call(f32[1]{0:T(128)S(6)} %exp2.16.damp_ref, f32[1,192,128]{2,1,0:T(8,128)} %shard_map.37.packed_ref), custom_call_target="tpu_custom_call" | custom-call | tf_op jit(solution)/shard_map/pallas_call | solution.py:125
  74.4 12.5 %shard_map.39 = f32[8,192,192]{2,1,0:T(8,128)} custom-call(f32[1,192,128]{2,1,0:T(8,128)} %shard_map.38.packed_ref), custom_call_target="tpu_custom_call" | custom-call | tf_op jit(solution)/shard_map/pallas_call | solution.py:410
  86.9 2.7 %copy.6 = f32[8,192,192]{2,1,0:T(8,128)} copy(f32[8,192,192]{2,1,0:T(8,128)} %shard_map.39) | data formatting | bytes 2359296

commit v2 on v1

--- a/solution.py
+++ b/solution.py
@@ -36,40 +36,57 @@
     return lax.dot_general(a, b, (((1,), (1,)), ((), ())), precision=HIGH, preferred_element_type=jnp.float32)
 
 
+PANEL = 8
+
+
+def inverse_factor(block):
+    lane = lax.broadcasted_iota(jnp.int32, (PANEL, BLK), 1)
+    sub = lax.broadcasted_iota(jnp.int32, (PANEL, BLK), 0)
+    groups = BLK // PANEL
+    each = range(PANEL)
+    parts = [block[PANEL * g : PANEL * g + PANEL] for g in range(groups)]
+    whole = (PANEL, BLK)
+    for p in range(groups):
+        first = PANEL * p
+        columns = {g: [jnp.broadcast_to(parts[g][:, first + j : first + j + 1], whole) for j in each] for g in range(p, groups)}
+        low = [[jnp.broadcast_to(columns[p][j][i : i + 1], whole) for j in range(i + 1)] for i in each]
+        inside = (lane >= first) & (lane < first + PANEL)
+        rows = []
+        for i in each:
+            own = jnp.where(inside, jnp.where(lane == first + i, 1.0, 0.0), jnp.broadcast_to(parts[p][i : i + 1], whole))
+            rows.append(own)
+        scale = []
+        for k in each:
+            inverse = 1.0 / low[k][k]
+            scale.append(inverse)
+            raw = {i: low[i][k] for i in range(k, PANEL)}
+            for i in range(k + 1, PANEL):
+                ratio = raw[i] * inverse
+                for j in range(k + 1, i + 1):
+                    low[i][j] = low[i][j] - ratio * raw[j]
+                rows[i] = rows[i] - ratio * rows[k]
+                low[i][k] = ratio
+        done = jnp.zeros(whole, jnp.float32)
+        for i in each:
+            done = jnp.where((sub == i) & (lane <= first + i), rows[i] * lax.rsqrt(low[i][i]), done)
+        if p + 1 < groups:
+            solved = [None] * PANEL
+            for k in reversed(each):
+                value = rows[k] * scale[k]
+                for i in range(k + 1, PANEL):
+                    value = value - low[i][k] * solved[i]
+                solved[k] = value
+            for g in range(p + 1, groups):
+                terms = [columns[g][j] * solved[j] for j in each]
+                while len(terms) > 1:
+                    terms = [a + b for a, b in zip(terms[::2], terms[1::2])]
+                parts[g] = jnp.where(inside, 0.0, parts[g]) - terms[0]
+        parts[p] = done
+    return jnp.concatenate(parts, axis=0)
+
+
 def inverse_factors(blocks):
-    lane = lax.broadcasted_iota(jnp.int32, (8, BLK), 1)
-    sub = lax.broadcasted_iota(jnp.int32, (8, BLK), 0)
-    sub1 = lax.broadcasted_iota(jnp.int32, (8, 1), 0)
-    groups = BLK // 8
-    held = [[block[8 * g : 8 * g + 8] for g in range(groups)] for block in blocks]
-    for k in range(BLK):
-        own, spot = divmod(k, 8)
-        is_k = lane == k
-        for parts in held:
-            row = parts[own][spot : spot + 1, :]
-            scale = 1.0 / row[:, k : k + 1]
-            row = jnp.where(is_k[:1], 1.0, row) * scale
-            for g in range(own, groups):
-                part = parts[g]
-                column = part[:, k : k + 1]
-                if g == own:
-                    if spot == 7:
-                        continue
-                    column = jnp.where(sub1 > spot, column, 0.0)
-                    kept = jnp.where(is_k & (sub > spot), 0.0, part)
-                else:
-                    kept = jnp.where(is_k, 0.0, part)
-                parts[g] = kept - column * row
-    out = []
-    for parts in held:
-        rows = []
-        for g in range(groups):
-            ids = sub + 8 * g
-            pivot = jnp.sum(jnp.where(lane == ids, parts[g], 0.0), axis=1, keepdims=True)
-            unit = jnp.where(lane < ids, parts[g], jnp.where(lane == ids, 1.0, 0.0))
-            rows.append(unit * (1.0 / jnp.sqrt(pivot)))
-        out.append(jnp.concatenate(rows, axis=0))
-    return out
+    return [inverse_factor(block) for block in blocks]
 
 
 def unpack_even(got):
@@ -147,11 +164,9 @@
 HALF = BLK // 2
 FAR_FIRST = (2, 1, 3, 0)
 ORDERS = ((0, 1, 2), (1, 2, 0), (2, 0, 1))
-AHEAD = 2
-VISITS = sorted(
-    ((a, b) for a in range(RING) for b in range(RING)),
-    key=lambda s: ((s[0] != 2) + (s[1] != 2), (s[0] == 0) + (s[1] == 0)),
-)
+AHEAD = 6
+LAG = 4
+VISITS = ((2, 2), (2, 1), (1, 2), (2, 3), (3, 2), (2, 0), (0, 2), (1, 1), (1, 3), (3, 1), (3, 3), (1, 0), (3, 0), (0, 1), (0, 3), (0, 0))
 
 
 def place():
@@ -165,6 +180,10 @@
     spot[axis] = (spot[axis] + step) % RING
     x, y, z, core = spot
     return {"head": (x * 2 + y // 2) * 2 + core, "dp": y % 2 * RING + z}
+
+
+def slots_of(level, part):
+    return RING ** (1 + (part == 2)) if level == 0 else RING
 
 
 class Stage:
@@ -174,6 +193,7 @@
         self.axis = ORDERS[part][level]
         self.free = ORDERS[part][level + 1 :]
         self.to = [neighbour(self.axis, 1), neighbour(self.axis, -1)]
+        self.slots = slots_of(level, part)
 
     def pick(self, block, sub):
         spot = [sub.get(a, pl.ds(0, RING)) if a in self.free else pl.ds(0, 1) for a in range(3)]
@@ -183,12 +203,12 @@
     def rows(self, half):
         return (pl.ds(self.part * BLK + half * HALF, HALF),)
 
-    def far_copy(self, d, sub):
+    def far_copy(self, d, sub, slot=0):
         return remote(
             self.acc.at[self.pick(2, sub) + self.rows(d)],
             self.far.at[(d,) + self.pick(0, sub)],
             self.sem_send.at[0, d],
-            self.sem_far.at[d],
+            self.sem_far.at[d, slot],
             self.to[d],
         )
 
@@ -197,7 +217,7 @@
             self.acc.at[self.pick((1, 3)[d], sub) + self.rows(1 - d)],
             self.near.at[(d,) + self.pick(0, sub) + (pl.ds((1 - d) * HALF, HALF),)],
             self.sem_send.at[1, d],
-            self.sem_near.at[d, RING],
+            self.sem_near.at[d, self.slots],
             self.to[d],
         )
 
@@ -215,14 +235,11 @@
             return [(0, {})]
         return [(g, {self.free[0]: pl.ds(g, 1)}) for g in FAR_FIRST]
 
-    def relay(self, d, group, sub):
+    def relay(self, d, sub):
         mine = self.pick((1, 3)[d], sub) + self.rows(d)
         self.acc[mine] += self.far[(d,) + self.pick(0, sub)]
-        self.near_copy(d, sub, group).start()
-
-    def settle(self, group, sub):
-        for d in (0, 1):
-            self.near_copy(d, sub, group).wait_recv()
+
+    def settle(self, sub):
         mine = self.pick(0, sub)
         size = [RING if len(self.free) > 1 and a == self.free[1] else 1 for a in range(3)]
         for i in range(max(size)):
@@ -245,16 +262,18 @@
     return tuple(RING if a in free else 1 for a in range(3))
 
 
-def scatter_kernel(rows_ref, weights_ref, out_ref, acc, sent, got, wide, columns, *rest):
+def scatter_kernel(rows_ref, weights_ref, out_ref, acc, sent, got, mine, wide, columns, *rest):
     x, y, z, core = place()
     sem_in, sem_core = rest[-2:]
     stages = [[Stage(part, level, acc, *rest[5 * (3 * level + part) :][:5]) for part in range(3)] for level in range(3)]
     span = RING * HD
     partner = {"head": lax.axis_index("head") // 2 * 2 + 1 - core}
     count = len(VISITS)
+    index = {spot: i for i, spot in enumerate(VISITS)}
     trips = [(0, 0)]
     for i in range(count):
         trips += [(i + 1, 0)] * (i + 1 < count) + [(i, 1)]
+    turn = {trip: v for v, trip in enumerate(trips)}
 
     def fetch(v):
         i, own = trips[v]
@@ -262,7 +281,7 @@
         to_core = core if own else 1 - core
         first = ((to_x * 2 + to_y // 2) * 2 + to_core) * 8 + to_y % 2 * RING
         start = pl.multiple_of(first * HD, 2 * BLK)
-        slot = v % (AHEAD + 1)
+        slot = v % AHEAD
         return pltpu.make_async_copy(rows_ref.at[:, pl.ds(start, span)], columns.at[slot], sem_in.at[slot])
 
     for v in range(AHEAD):
@@ -270,64 +289,88 @@
     wide[...] = jnp.broadcast_to(weights_ref[...], wide.shape)
 
     def multiply(v, out):
-        if v + AHEAD < len(trips):
-            fetch(v + AHEAD).start()
-        fetch(v).wait()
-
-        def pair(i, carry):
-            start = pl.multiple_of(i * 2 * HD, 2 * BLK)
+        for i in range(RING // 2):
             even = (2 * i + RING - z) % RING
-            store_pair(columns[v % (AHEAD + 1), :, pl.ds(start, 2 * HD)], wide[...], out, even, (even + 1) % RING)
-            return carry
-
-        lax.fori_loop(0, RING // 2, pair, 0, unroll=True)
+            store_pair(columns[v % AHEAD, :, 2 * i * HD : 2 * (i + 1) * HD], wide[...], out, even, (even + 1) % RING)
 
     def exchange(i):
         return remote(sent.at[i], got.at[i], sem_core.at[0, i], sem_core.at[1, i], partner)
 
-    def release(i):
+    def spots(i):
         a, b = VISITS[i]
-        exchange(i).wait_recv()
-
-        def add(m, carry):
-            acc[a, b, m] += got[i, m]
-            return carry
-
-        lax.fori_loop(0, RING, add, 0)
-        spots = ({1: pl.ds(b, 1)}, {0: pl.ds(a, 1)}, {0: pl.ds(a, 1), 1: pl.ds(b, 1)})
-        for stage, at, sub in zip(stages[0], (a, b, None), spots):
-            for d in (0, 1):
-                if at in (2, None):
-                    stage.far_copy(d, sub).start()
+        return ((a, {1: pl.ds(b, 1)}, b), (b, {0: pl.ds(a, 1)}, a), (None, {0: pl.ds(a, 1), 1: pl.ds(b, 1)}, RING * a + b))
+
+    relays = {}
+    for i in range(count):
+        for part, (at, sub, slot) in enumerate(spots(i)):
             for d in (0, 1):
                 if at in ((1, 3)[d], None):
-                    stage.direct_copy(d, sub).start()
-
-    for v, (i, own) in enumerate(trips):
-        if own:
-            multiply(v, acc.at[VISITS[i]])
-            if i:
-                release(i - 1)
-        else:
-            multiply(v, sent.at[i])
-            if v == 0:
-                greet([partner] + [to for stage in stages[0] for to in stage.to])
-            exchange(i).start()
-    release(count - 1)
+                    source = VISITS[i] if at is None else tuple(2 if n == part else VISITS[i][n] for n in range(2))
+                    when = max(i + 2, index[source] + LAG)
+                    relays.setdefault(when, []).append((stages[0][part], d, sub, slot))
+
+    for r in range(-1, max(relays) + 1):
+        now = [turn[trip] for trip in ((r + 1, 0), (r, 1)) if trip in turn]
+        for v in now:
+            fetch(v).wait()
+        if 1 <= r <= count:
+            exchange(r - 1).wait_recv()
+        moved = relays.get(r, [])
+        for stage, d, sub, slot in moved:
+            stage.far_copy(d, sub, slot).wait_recv()
+        for v in now:
+            i, own = trips[v]
+            multiply(v, mine.at[i % 2] if own else sent.at[i])
+        if 1 <= r <= count:
+            a, b = VISITS[r - 1]
+            acc[a, b] = mine[(r - 1) % 2] + got[r - 1]
+        for stage, d, sub, slot in moved:
+            stage.relay(d, sub)
+        if r == -1:
+            greet([partner] + [to for stage in stages[0] for to in stage.to])
+        if r + 1 < count:
+            exchange(r + 1).start()
+        for v in now:
+            if v + AHEAD < len(trips):
+                fetch(v + AHEAD).start()
+        if 1 <= r <= count:
+            for stage, (at, sub, slot) in zip(stages[0], spots(r - 1)):
+                for d in (0, 1):
+                    if at in (2, None):
+                        stage.far_copy(d, sub, slot).start()
+        for stage, d, sub, slot in moved:
+            stage.near_copy(d, sub, slot).start()
+        if 1 <= r <= count:
+            for stage, (at, sub, slot) in zip(stages[0], spots(r - 1)):
+                for d in (0, 1):
+                    if at in ((1, 3)[d], None):
+                        stage.direct_copy(d, sub).start()
+
     for level in range(3):
         now = stages[level]
-        for stage in now:
-            for d in (0, 1):
-                stage.far_copy(d, {}).wait_recv()
-                for group, sub in stage.groups():
-                    stage.relay(d, group, sub)
+        if level:
+            for stage in now:
+                for d in (0, 1):
+                    stage.far_copy(d, {}).wait_recv()
+                    for group, sub in stage.groups():
+                        stage.relay(d, sub)
+                        stage.near_copy(d, sub, group).start()
         for stage in now:
             for d in (0, 1):
                 stage.direct_copy(d, {}).wait_recv()
         for n in range(len(now[0].groups())):
             for part in range(3):
                 group, sub = now[part].groups()[n]
-                now[part].settle(group, sub)
+                if level or part == 0:
+                    arrivals = [(sub, group)]
+                elif part == 1:
+                    arrivals = [({0: pl.ds(a, 1)}, a) for a in range(RING) if n == 0]
+                else:
+                    arrivals = [({0: pl.ds(group, 1), 1: pl.ds(b, 1)}, RING * group + b) for b in range(RING)]
+                for at, slot in arrivals:
+                    for d in (0, 1):
+                        now[part].near_copy(d, at, slot).wait_recv()
+                now[part].settle(sub)
                 if level < 2:
                     later = stages[level + 1][part]
                     if group == 2:
@@ -354,8 +397,8 @@
             rings += [
                 pltpu.VMEM((2,) + shape + (HALF, lanes), f32),
                 pltpu.VMEM((2,) + shape + (BLK, lanes), f32),
-                pltpu.SemaphoreType.DMA((2,)),
-                pltpu.SemaphoreType.DMA((2, RING + 1)),
+                pltpu.SemaphoreType.DMA((2, slots_of(level, part))),
+                pltpu.SemaphoreType.DMA((2, slots_of(level, part) + 1)),
                 pltpu.SemaphoreType.DMA((3, 2)),
             ]
     return pl.pallas_call(
@@ -367,10 +410,11 @@
             pltpu.VMEM((RING, RING, RING, rows, lanes), f32),
             pltpu.VMEM((len(VISITS), RING, rows, lanes), f32),
             pltpu.VMEM((len(VISITS), RING, rows, lanes), f32),
+            pltpu.VMEM((2, RING, rows, lanes), f32),
             pltpu.VMEM((tokens, 2 * HD), projected.dtype),
-            pltpu.VMEM((AHEAD + 1, tokens, RING * HD), projected.dtype),
+            pltpu.VMEM((AHEAD, tokens, RING * HD), projected.dtype),
             *rings,
-            pltpu.SemaphoreType.DMA((AHEAD + 1,)),
+            pltpu.SemaphoreType.DMA((AHEAD,)),
             pltpu.SemaphoreType.DMA((2, len(VISITS))),
         ],
         compiler_params=pltpu.CompilerParams(collective_id=0, has_side_effects=True, vmem_limit_bytes=60 << 20),

time: 90.1 us -> 83.5 us (0.927)
  Pallas kernels: 83.5 us -> 77.2 us
    pallas_call x1, Pallas kernels: 19.2 us -> 10.9 us  [whiten(): pl.pallas_call(functools.partial(whiten_kernel, total, count), in_specs=[...]
    pallas_call x1, Pallas kernels: 51.8 us -> 53.7 us  [gram_sums(): pl.pallas_call(scatter_kernel, in_specs=[pl.BlockSpec(memory_space=pl.ANY...]
where the time goes in v2:
time: 83.5 us; the launch traced here: 83.2 us
  Pallas kernels  77.2 us (92%)
  local copies, waits for them, and re-layouts  4.66 us (6%)
    pallas_call x1, Pallas kernels, gram_sums(): pl.pallas_call(scatter_kernel, in_specs=[pl.BlockSpec(memory_space=pl.ANY...  53.7 us
    pallas_call x1, Pallas kernels, gather(): pl.pallas_call(functools.partial(gather_kernel, n_dp, share), in_specs=[p...  12.5 us
    pallas_call x1, Pallas kernels, whiten(): pl.pallas_call(functools.partial(whiten_kernel, total, count), in_specs=[...  10.9 us
    unnamed x1, local copies, waits for them, and re-layouts  2.65 us

profile of v2, /device:TPU:0, one launch (start us, length us, event | category | flops | bytes accessed | tf_op | source)
XLA Modules:
  0.0 83.2 jit_solution(1369288625316873591)
XLA Ops:
  0.0 1.2 %dynamic_slice.3 = s32[1]{0:T(128)} dynamic-slice(s32[128]{0:T(128)} %param.5, s32[]{:T(128)S(6)} %select_n.3), dynamic_slice_sizes={1} | dynamic-slice | bytes 12 | tf_op jit(solution)/shard_map/dynamic_slice | solution.py:476
  1.9 0.7 exponential_convert_fusion
  2.6 0.8 broadcast_in_dim.4.weights_ref
  3.4 53.7 %shard_map.37.packed_ref = f32[1,192,128]{2,1,0:T(8,128)} custom-call(bf16[384,24576]{1,0:T(8,128)(2,1)} %rows_ref.1, bf16[384,1]{1,0:T(8,128)(2,1)} %broadcast_in_dim.4.weights_ref), custom_call_target="tpu_custom_call" | custom-call | tf_op jit(solution)/shard_map/pallas_call | solution.py:404
  57.1 10.9 %shard_map.38.packed_ref = f32[1,192,128]{2,1,0:T(8,128)} custom-call(f32[1]{0:T(128)S(6)} %exp2.16.damp_ref, f32[1,192,128]{2,1,0:T(8,128)} %shard_map.37.packed_ref), custom_call_target="tpu_custom_call" | custom-call | tf_op jit(solution)/shard_map/pallas_call | solution.py:142
  68.0 12.5 %shard_map.39 = f32[8,192,192]{2,1,0:T(8,128)} custom-call(f32[1,192,128]{2,1,0:T(8,128)} %shard_map.38.packed_ref), custom_call_target="tpu_custom_call" | custom-call | tf_op jit(solution)/shard_map/pallas_call | solution.py:454
  80.6 2.7 %copy.6 = f32[8,192,192]{2,1,0:T(8,128)} copy(f32[8,192,192]{2,1,0:T(8,128)} %shard_map.39) | data formatting | bytes 2359296

commit v3 on v2

v3 whole, which is shorter than its diff:
```python
import functools

import jax
import jax.numpy as jnp
from jax import lax
from jax.experimental import pallas as pl
from jax.experimental.pallas import tpu as pltpu
from jax.sharding import PartitionSpec as P

HD = 192
BLK = HD // 3
HIGH = lax.Precision.HIGHEST


def store_pair(rows, wide, out, at, after):
    weighted = rows * wide
    contract = (((0,), (0,)), ((), ()))
    width = 4 * BLK
    first = lax.dot_general(rows[:, :width], weighted[:, :width], contract, preferred_element_type=jnp.float32)
    second = lax.dot_general(rows[:, -width:], weighted[:, -width:], contract, preferred_element_type=jnp.float32)
    two = 2 * BLK
    lanes = lax.broadcasted_iota(jnp.int32, (BLK, two), 1)
    corner = pltpu.roll(first[two : two + BLK, two:], BLK, 1)
    out[at, :BLK, :] = jnp.where(lanes < BLK, first[:BLK, :two], corner)
    out[at, BLK:, :] = first[BLK:HD, :two]
    out[after, :two, :] = second[BLK : BLK + two, two:]
    corner = pltpu.roll(second[BLK:two, :two], BLK, 1)
    out[after, two:, :] = jnp.where(lanes < BLK, corner, second[HD:, two:])


def dot(a, b):
    return lax.dot_general(a, b, (((1,), (0,)), ((), ())), precision=HIGH, preferred_element_type=jnp.float32)


def dot_t(a, b):
    return lax.dot_general(a, b, (((1,), (1,)), ((), ())), precision=HIGH, preferred_element_type=jnp.float32)


PANEL = 8


def inverse_factor(block):
    lane = lax.broadcasted_iota(jnp.int32, (PANEL, BLK), 1)
    sub = lax.broadcasted_iota(jnp.int32, (PANEL, BLK), 0)
    groups = BLK // PANEL
    each = range(PANEL)
    whole = (PANEL, BLK)
    parts = [block[PANEL * g : PANEL * g + PANEL] for g in range(groups)]

    def spread(part, at):
        return [jnp.broadcast_to(part[:, at + j : at + j + 1], whole) for j in each]

    def total(terms):
        while len(terms) > 1:
            terms = [a + b for a, b in zip(terms[::2], terms[1::2])]
        return terms[0]

    own = spread(parts[0], 0)
    for p in range(groups):
        first = PANEL * p
        columns = {g: spread(parts[g], first) for g in range(p + 1, groups)}
        ahead = spread(parts[p + 1], first + PANEL) if p + 1 < groups else None
        low = [[jnp.broadcast_to(own[j][i : i + 1], whole) for j in range(i + 1)] for i in each]
        inside = (lane >= first) & (lane < first + PANEL)
        rows = [
            jnp.where(inside, jnp.where(lane == first + i, 1.0, 0.0), jnp.broadcast_to(parts[p][i : i + 1], whole)) for i in each
        ]
        scale = []
        for k in each:
            inverse = 1.0 / low[k][k]
            scale.append(inverse)
            raw = {i: low[i][k] for i in range(k, PANEL)}
            for i in range(k + 1, PANEL):
                ratio = raw[i] * inverse
                for j in range(k + 1, i + 1):
                    low[i][j] = low[i][j] - ratio * raw[j]
                rows[i] = rows[i] - ratio * rows[k]
                low[i][k] = ratio
        done = jnp.zeros(whole, jnp.float32)
        for i in each:
            done = jnp.where((sub == i) & (lane <= first + i), rows[i] * lax.rsqrt(low[i][i]), done)
        if p + 1 < groups:
            cross = columns[p + 1]
            lifted = []
            for k in each:
                value = cross[k]
                for j in range(k):
                    value = value - low[k][j] * lifted[j]
                lifted.append(value)
            scaled = [lifted[k] * scale[k] for k in each]
            own = [
                ahead[j] - total([scaled[k] * jnp.broadcast_to(lifted[k][j : j + 1], whole) for k in each]) for j in each
            ]
            solved = [None] * PANEL
            for k in reversed(each):
                value = rows[k] * scale[k]
                for i in range(k + 1, PANEL):
                    value = value - low[i][k] * solved[i]
                solved[k] = value
            for g in range(p + 1, groups):
                parts[g] = jnp.where(inside, 0.0, parts[g]) - total([columns[g][j] * solved[j] for j in each])
        parts[p] = done
    return jnp.concatenate(parts, axis=0)


def unpack_even(got):
    two = 2 * BLK
    return got[:BLK, :BLK], got[BLK:two, BLK:], got[:BLK, BLK:], got[BLK:, :BLK], got[two:, BLK:]


def unpack_odd(got):
    two = 2 * BLK
    return got[two:, :BLK], got[BLK:two, :BLK], got[two:, BLK:], got[:BLK, :].T, got[BLK:two, BLK:].T


def remote(src, dst, send, recv, device):
    return pltpu.make_async_remote_copy(
        src_ref=src, dst_ref=dst, send_sem=send, recv_sem=recv, device_id=device, device_id_type=pl.DeviceIdType.MESH
    )


def greet(devices):
    barrier = pltpu.get_barrier_semaphore()
    for device in devices:
        pl.semaphore_signal(barrier, inc=1, device_id=device, device_id_type=pl.DeviceIdType.MESH)
    pl.semaphore_wait(barrier, len(devices))


RING = 4
HALF = BLK // 2
FAR_FIRST = (2, 1, 3, 0)
ORDERS = ((0, 1, 2), (1, 2, 0), (2, 0, 1))
AHEAD = 6
VISIT_US = 1.0
TAIL_US = 0.2
HOP_US = 2.5
LINK_RATE = 46.6e3
VISITS = ((2, 2), (2, 1), (1, 2), (2, 3), (3, 2), (2, 0), (0, 2), (1, 0), (3, 0), (0, 0), (1, 1), (3, 3), (1, 3), (3, 1), (0, 1), (0, 3))


def place():
    head = lax.axis_index("head")
    dp = lax.axis_index("dp")
    return head // 4, head // 2 % 2 * 2 + dp // RING, dp % RING, head % 2


def neighbour(axis, step):
    spot = list(place())
    spot[axis] = (spot[axis] + step) % RING
    x, y, z, core = spot
    return {"head": (x * 2 + y // 2) * 2 + core, "dp": y % 2 * RING + z}


class First:
    def __init__(self, part, acc, far, near, sem_far, sem_near, sem_send):
        self.part, self.level, self.acc, self.far, self.near = part, 0, acc, far, near
        self.size = far.shape[1] * BLK * 2 * BLK * 4
        self.sem_far, self.sem_near, self.sem_send = sem_far, sem_near, sem_send
        self.to = [neighbour(part, 1), neighbour(part, -1)]
        self.rows = pl.ds(part * BLK, BLK)

    def parity(self, slot):
        return (slot + slot // RING) % 2

    def visit(self, block, slot):
        return ((block, slot), (slot, block), (slot // RING, slot % RING))[self.part]

    def slot(self, visit):
        a, b = visit
        return (b, a, RING * a + b)[self.part]

    def block(self, visit):
        return (visit[0], visit[1], None)[self.part]

    def at(self, block, slot):
        return self.visit(block, slot) + (pl.ds(block, 1) if self.part == 2 else pl.ds(0, RING), self.rows)

    def whole(self, block):
        spot = [pl.ds(0, RING)] * 3
        spot[self.part] = pl.ds(block, 1)
        return self.acc.at[tuple(spot) + (self.rows,)]

    def far_copy(self, slot):
        return remote(
            self.acc.at[self.at(2, slot)], self.far.at[slot], self.sem_send.at[0], self.sem_far.at[slot], self.to[self.parity(slot)]
        )

    def near_copy(self, d, slot):
        return remote(
            self.acc.at[self.at((1, 3)[d], slot)], self.near.at[d, slot], self.sem_send.at[1 + d], self.sem_near.at[d, slot], self.to[d]
        )

    def relay(self, slot):
        self.acc[self.at((1, 3)[self.parity(slot)], slot)] += self.far[slot]

    def members(self, group):
        return ([group], list(range(RING)), [RING * group + b for b in range(RING)])[self.part]

    def settle(self, group):
        for slot in self.members(group):
            if self.part == 1:
                self.acc[slot, 0, group, self.rows] += self.near[0, slot, group] + self.near[1, slot, group]
            else:
                self.acc[self.at(0, slot)] += self.near[0, slot] + self.near[1, slot]

    def finish(self):
        for sem, block in enumerate((2, 1, 3)):
            whole = self.whole(block)
            remote(whole, whole, self.sem_send.at[sem], self.sem_far.at[0], self.to[0]).wait_send()


class Later:
    def __init__(self, part, level, acc, far, near, sem_far, sem_near, sem_send):
        self.part, self.level, self.acc, self.far, self.near = part, level, acc, far, near
        self.size = (1 if level == 2 else RING) * HALF * 2 * BLK * 4
        self.sem_far, self.sem_near, self.sem_send = sem_far, sem_near, sem_send
        self.axis = ORDERS[part][level]
        self.free = ORDERS[part][level + 1 :]
        self.to = [neighbour(self.axis, 1), neighbour(self.axis, -1)]

    def pick(self, block, group):
        spot = [pl.ds(0, 1)] * 3
        for axis in self.free:
            spot[axis] = pl.ds(0, RING) if group is None else pl.ds(group, 1)
        spot[self.axis] = pl.ds(block, 1)
        return tuple(spot)

    def rows(self, half):
        return (pl.ds(self.part * BLK + half * HALF, HALF),)

    def copy(self, src, dst, send, recv, d):
        return remote(self.acc.at[src], dst, self.sem_send.at[send, d], recv, self.to[d])

    def far_copy(self, d):
        return self.copy(self.pick(2, None) + self.rows(d), self.far.at[(d,) + self.pick(0, None)], 0, self.sem_far.at[d], d)

    def direct_copy(self, d):
        half = self.near.at[(d,) + self.pick(0, None) + (pl.ds((1 - d) * HALF, HALF),)]
        return self.copy(self.pick((1, 3)[d], None) + self.rows(1 - d), half, 1, self.sem_near.at[d, RING], d)

    def near_copy(self, d, group):
        half = self.near.at[(d,) + self.pick(0, group) + (pl.ds(d * HALF, HALF),)]
        return self.copy(self.pick((1, 3)[d], group) + self.rows(d), half, 2, self.sem_near.at[d, group or 0], d)

    def groups(self):
        return FAR_FIRST if self.free else (0,)

    def relay(self, d):
        self.acc[self.pick((1, 3)[d], None) + self.rows(d)] += self.far[(d,) + self.pick(0, None)]

    def settle(self, group):
        spot = self.pick(0, group)
        self.acc[spot + (pl.ds(self.part * BLK, BLK),)] += self.near[(0,) + spot] + self.near[(1,) + spot]

    def finish(self):
        for d in (0, 1):
            for copy in (self.far_copy(d), self.direct_copy(d), self.near_copy(d, None)):
                copy.wait_send()


def scatter_kernel(rows_ref, weights_ref, out_ref, acc, sent, got, mine, wide, columns, *rest):
    x, y, z, core = place()
    sem_in, sem_core = rest[-2:]
    stages = [[(First(part, acc, *refs) if level == 0 else Later(part, level, acc, *refs)) for part in range(3) for refs in [rest[5 * (3 * level + part) :][:5]]] for level in range(3)]
    span = RING * HD
    partner = {"head": lax.axis_index("head") // 2 * 2 + 1 - core}
    count = len(VISITS)
    trips = [(0, 0)]
    for i in range(count):
        trips += [(i + 1, 0)] * (i + 1 < count) + [(i, 1)]
    turn = {trip: v for v, trip in enumerate(trips)}

    def fetch(v):
        i, own = trips[v]
        to_x, to_y = (x + VISITS[i][0]) % RING, (y + VISITS[i][1]) % RING
        to_core = core if own else 1 - core
        first = ((to_x * 2 + to_y // 2) * 2 + to_core) * 8 + to_y % 2 * RING
        start = pl.multiple_of(first * HD, 2 * BLK)
        slot = v % AHEAD
        return pltpu.make_async_copy(rows_ref.at[:, pl.ds(start, span)], columns.at[slot], sem_in.at[slot])

    for v in range(AHEAD):
        fetch(v).start()
    for k in range(wide.shape[0] // (2 * BLK)):
        power = weights_ref[pl.ds(2 * BLK * k, 2 * BLK)].reshape(1, 2 * BLK)
        weight = jnp.where(power % 2 == 1, 2.0, 1.0) * jnp.where(power >= 2, 4.0, 1.0)
        block = jnp.broadcast_to(weight, (2 * BLK, 2 * BLK)).T.astype(wide.dtype)
        for j in range(3):
            wide[2 * BLK * k : 2 * BLK * (k + 1), 2 * BLK * j : 2 * BLK * (j + 1)] = block

    def multiply(v, out):
        for i in range(RING // 2):
            even = (2 * i + RING - z) % RING
            store_pair(columns[v % AHEAD, :, 2 * i * HD : 2 * (i + 1) * HD], wide[...], out, even, (even + 1) % RING)

    def exchange(i):
        return remote(sent.at[i], got.at[i], sem_core.at[0, i], sem_core.at[1, i], partner)

    def add(i):
        a, b = VISITS[i]
        acc[a, b] = mine[i % 2] + got[i]

    events = []
    links = {}

    def message(copy, stage, d, rank, key, pieces=1):
        links[key] = (copy, (ORDERS[stage.part][stage.level], d), stage.size // pieces, rank)
        return key

    def plan(name, needs, arrivals, work, sends):
        events.append((name, needs, arrivals, work, sends))

    for i, spot in enumerate(VISITS):
        sends = []
        for s in stages[0]:
            slot = s.slot(spot)
            if s.block(spot) in (2, None):
                sends.append(message(s.far_copy(slot), s, s.parity(slot), 0, (s, "far", slot)))
            side = 1 - s.parity(slot)
            if s.block(spot) in ((1, 3)[side], None):
                sends.append(message(s.near_copy(side, slot), s, side, 2, (s, "near", side, slot)))
        plan(spot, [], [i], functools.partial(add, i), sends)
    for s, t, u in zip(*stages):
        for slot in range(s.near.shape[1]):
            d = s.parity(slot)
            send = message(s.near_copy(d, slot), s, d, 1, (s, "near", d, slot))
            plan((s, "relay", slot), [s.visit((1, 3)[d], slot)], [(s, "far", slot)], functools.partial(s.relay, slot), [send])
        for group in FAR_FIRST:
            slots = s.members(group)
            arrivals = [(s, "near", d, slot) for d in (0, 1) for slot in slots]
            sends = []
            if group == 2:
                sends = [message(t.far_copy(d), t, d, 0, (t, "far", d)) for d in (0, 1)]
            elif group:
                sends = [message(t.direct_copy(group // 2), t, group // 2, 2, (t, "direct", group // 2))]
            plan((s, group), [s.visit(0, slot) for slot in slots], arrivals, functools.partial(s.settle, group), sends)
        for before, now, after in ((s, t, u), (t, u, None)):
            for d in (0, 1):
                sends = [message(now.near_copy(d, g), now, d, 1, (now, "near", d, g), len(now.groups())) for g in now.groups()]
                plan((now, "relay", d), [(before, (1, 3)[d])], [(now, "far", d)], functools.partial(now.relay, d), sends)
            for g in now.groups():
                arrivals = [(now, kind, d, g) for d in (0, 1) for kind in ("near",)] + [(now, "direct", d) for d in (0, 1)]
                sends = []
                if after and g == 2:
                    sends = [message(after.far_copy(d), after, d, 0, (after, "far", d)) for d in (0, 1)]
                elif after and g:
                    sends = [message(after.direct_copy(g // 2), after, g // 2, 2, (after, "direct", g // 2))]
                plan((now, g), [(before, 0)], arrivals, functools.partial(now.settle, g), sends)

    done, waited, due, free = set(), set(), {}, {}
    pending = list(events)
    clock = 0.0
    r = -1
    while pending:
        now = [turn[trip] for trip in ((r + 1, 0), (r, 1)) if trip in turn]
        ready = []
        for event in list(pending):
            name, needs, arrivals, _, _ = event
            if isinstance(arrivals[0], int):
                fit = arrivals[0] == r - 1
            else:
                fit = all(n in done for n in needs) and all(due.get(m, 1e9) <= clock for m in arrivals)
            if fit:
                ready.append(event)
                pending.remove(event)
                done.add(name)
        for v in now:
            fetch(v).wait()
        for _, _, arrivals, _, _ in ready:
            for m in arrivals:
                if m not in waited:
                    waited.add(m)
                    (exchange(m) if isinstance(m, int) else links[m][0]).wait_recv()
        for v in now:
            i, own = trips[v]
            multiply(v, mine.at[i % 2] if own else sent.at[i])
        for _, _, _, work, _ in ready:
            work()
        if r == -1:
            greet([partner] + [to for stage in stages[0] for to in stage.to])
        if r + 1 < count:
            exchange(r + 1).start()
        for v in now:
            if v + AHEAD < len(trips):
                fetch(v + AHEAD).start()
        clock += VISIT_US if r <= count else TAIL_US
        for m in sorted((m for event in ready for m in event[4]), key=lambda m: links[m][3]):
            copy, link, size, _ = links[m]
            copy.start()
            free[link] = max(free.get(link, 0.0), clock) + size / LINK_RATE + 0.08
            due[m] = free[link] + HOP_US
        r += 1
    out_ref[0] = acc[0, 0, 0]
    for i in range(count):
        exchange(i).wait_send()
    for level in stages:
        for stage in level:
            stage.finish()


def gram_sums(projected, weights):
    tokens, width = projected.shape
    rows, lanes = HD, 2 * BLK
    f32 = jnp.float32
    rings = []
    for level in range(3):
        for part in range(3):
            if level:
                free = ORDERS[part][level + 1 :]
                far = (2,) + tuple(RING if a in free else 1 for a in range(3)) + (HALF, lanes)
                near = far[:-2] + (BLK, lanes)
                sems = (2,), (2, RING + 1), (3, 2)
            else:
                slots, each = ((RING, RING), (RING, RING), (RING * RING, 1))[part]
                far = (slots, each, BLK, lanes)
                near = (2,) + far
                sems = (slots,), (2, slots), (3,)
            rings += [pltpu.VMEM(far, f32), pltpu.VMEM(near, f32), *map(pltpu.SemaphoreType.DMA, sems)]
    return pl.pallas_call(
        scatter_kernel,
        in_specs=[pl.BlockSpec(memory_space=pl.ANY), pl.BlockSpec(memory_space=pltpu.VMEM)],
        out_specs=pl.BlockSpec(memory_space=pltpu.VMEM),
        out_shape=jax.ShapeDtypeStruct((1, rows, lanes), f32),
        scratch_shapes=[
            pltpu.VMEM((RING, RING, RING, rows, lanes), f32),
            pltpu.VMEM((len(VISITS), RING, rows, lanes), f32),
            pltpu.VMEM((len(VISITS), RING, rows, lanes), f32),
            pltpu.VMEM((2, RING, rows, lanes), f32),
            pltpu.VMEM((tokens, 2 * HD), projected.dtype),
            pltpu.VMEM((AHEAD, tokens, RING * HD), projected.dtype),
            *rings,
            pltpu.SemaphoreType.DMA((AHEAD,)),
            pltpu.SemaphoreType.DMA((2, len(VISITS))),
        ],
        compiler_params=pltpu.CompilerParams(collective_id=0, has_side_effects=True, vmem_limit_bytes=60 << 20),
    )(projected, weights)


def fold(block):
    return jnp.concatenate((block[:HALF], block[HALF:]), axis=1)


def whiten_kernel(total, damp_ref, packed_ref, out_ref, sems):
    head, dp = lax.axis_index("head"), lax.axis_index("dp")
    n_dp = out_ref.shape[0]
    peers = [lax.rem(dp + o, n_dp) for o in range(1, n_dp)]
    two, early = 2 * BLK, HD // 2

    def share(part):
        rows = out_ref.at[dp, pl.ds(part * early, early)]
        return [remote(rows, rows, sems.at[0, part, o], sems.at[1, part, o], {"dp": peer}) for o, peer in enumerate(peers)]

    greet([{"dp": peer} for peer in peers])
    got = packed_ref[0] / total
    even = dp % 2 == 0
    a11, a22, a33, low, a32 = (jnp.where(even, a, b) for a, b in zip(unpack_even(got), unpack_odd(got)))
    diag = lax.broadcasted_iota(jnp.int32, (BLK, BLK), 0) == lax.broadcasted_iota(jnp.int32, (BLK, BLK), 1)
    trace = jnp.sum(jnp.where(diag, a11 + a22 + a33, 0.0), axis=(0, 1), keepdims=True)
    level = trace / HD + 1e-06
    power = damp_ref[head * n_dp + dp]
    damp = jnp.where(power % 2 == 1, 0.5, 1.0) * jnp.where(power >= 2, 0.25, 1.0)
    shift = jnp.where(diag, damp * level, 0.0)
    w11 = inverse_factor(a11 + shift)
    l1 = dot_t(low, w11)
    square = dot_t(l1, l1)
    below = dot(l1, w11)
    w22 = inverse_factor(a22 + shift - square[:BLK, :BLK])
    w21 = -dot(w22, below[:BLK])
    out_ref[dp, :BLK] = jnp.concatenate((w11, w22), axis=1)
    out_ref[dp, BLK:early] = fold(w21)
    for copy in share(0):
        copy.start()
    l32 = dot_t(a32 - square[BLK:, :BLK], w22)
    w33 = inverse_factor(a33 + shift - square[BLK:, BLK:] - dot_t(l32, l32))
    w31 = -dot(w33, below[BLK:] + dot(l32, w21))
    w32 = -dot(w33, dot(l32, w22))
    out_ref[dp, early:two] = fold(w33)
    out_ref[dp, two:] = jnp.concatenate((w31, w32), axis=1)
    for copy in share(1):
        copy.start()
    for part in (0, 1):
        for copy in share(part):
            copy.wait()


def whiten(packed, damp_exp, total, n_dp):
    return pl.pallas_call(
        functools.partial(whiten_kernel, total),
        in_specs=[pl.BlockSpec(memory_space=pltpu.SMEM), pl.BlockSpec(memory_space=pltpu.VMEM)],
        out_specs=pl.BlockSpec(memory_space=pltpu.VMEM),
        out_shape=jax.ShapeDtypeStruct((n_dp,) + packed.shape[1:], jnp.float32),
        scratch_shapes=[pltpu.SemaphoreType.DMA((2, 2, n_dp - 1))],
        compiler_params=pltpu.CompilerParams(collective_id=1, has_side_effects=True),
    )(damp_exp, packed)


def unpack_kernel(packed_ref, out_ref, whole, sems):
    two, early = 2 * BLK, HD // 2
    copies = []
    for m in range(packed_ref.shape[0]):
        whole[m, :BLK, :BLK] = packed_ref[m, :BLK, :BLK]
        whole[m, :BLK, BLK:] = jnp.zeros((BLK, two), jnp.float32)
        side = packed_ref[m, BLK:early]
        below = jnp.concatenate((side[:, :BLK], side[:, BLK:]), axis=0)
        right = lax.broadcasted_iota(jnp.int32, (BLK, two), 1) >= BLK
        whole[m, BLK:two, :two] = jnp.where(right, packed_ref[m, :BLK], jnp.concatenate((below, below), axis=1))
        whole[m, BLK:two, two:] = jnp.zeros((BLK, BLK), jnp.float32)
        whole[m, two:, :two] = packed_ref[m, two:]
        last = packed_ref[m, early:two]
        whole[m, two:, two:] = jnp.concatenate((last[:, :BLK], last[:, BLK:]), axis=0)
        copy = pltpu.make_async_copy(whole.at[m], out_ref.at[m], sems.at[m])
        copy.start()
        copies.append(copy)
    for copy in copies:
        copy.wait()


def unpack(packed):
    shape = (packed.shape[0], HD, HD)
    return pl.pallas_call(
        unpack_kernel,
        in_specs=[pl.BlockSpec(memory_space=pltpu.VMEM)],
        out_specs=pl.BlockSpec(memory_space=pl.ANY),
        out_shape=jax.ShapeDtypeStruct(shape, jnp.float32),
        scratch_shapes=[pltpu.VMEM(shape, jnp.float32), pltpu.SemaphoreType.DMA(shape[:1])],
    )(packed)


def on_device(projected, weight_exp, damp_exp):
    n_dp = lax.axis_size("dp")
    total = projected.shape[0] * lax.axis_size("head") * n_dp
    owned = gram_sums(projected, weight_exp)
    return unpack(whiten(owned, damp_exp, float(total), n_dp))


def solution(mesh):
    return jax.shard_map(
        on_device,
        mesh=mesh,
        in_specs=(P(("dp", "head"), None), P(("dp", "head")), P()),
        out_specs=P("head", None, None),
        check_vma=False,
    )
```

time: 83.5 us -> 74.4 us (0.89)
  local copies, waits for them, and re-layouts: 4.66 us -> 0 us
  Pallas kernels: 77.2 us -> 74 us
    pallas_call x2, Pallas kernels: 23.5 us -> 20.6 us  [the longest x1 18.2 us: whiten(): pl.pallas_call(functools.partial(whiten_kernel, total), in_specs=[pl.Bloc...]
    unnamed x1 -> x0, local copies, waits for them, and re-layouts: 2.65 us -> none
    dynamic_slice x1 -> x0, local copies, waits for them, and re-layouts: 1.24 us -> none  [on_device(): lax.dynamic_slice_in_dim(damp_exp, first, share, 0).astype(jnp.float32)]
where the time goes in v3:
time: 74.4 us; the launch traced here: 74.2 us
  Pallas kernels  74 us (99%)
    pallas_call x1, Pallas kernels, gram_sums(): pl.pallas_call(scatter_kernel, in_specs=[pl.BlockSpec(memory_space=pl.ANY...  53.4 us
    pallas_call x1, Pallas kernels, whiten(): pl.pallas_call(functools.partial(whiten_kernel, total), in_specs=[pl.Bloc...  18.2 us
    pallas_call x1, Pallas kernels, unpack(): pl.pallas_call(unpack_kernel, in_specs=[pl.BlockSpec(memory_space=pltpu.V...  2.47 us

profile of v3, /device:TPU:0, one launch (start us, length us, event | category | flops | bytes accessed | tf_op | source)
XLA Modules:
  0.0 74.2 jit_solution(16363145396249082599)
XLA Ops:
  0.0 53.4 %shard_map.37.packed_ref = f32[1,192,128]{2,1,0:T(8,128)} custom-call(bf16[384,24576]{1,0:T(8,128)(2,1)} %rows_ref.1, s32[384]{0:T(512)} %weights_ref.1), custom_call_target="tpu_custom_call" | custom-call | tf_op jit(solution)/shard_map/pallas_call | solution.py:419
  53.4 18.2 %shard_map.38.packed_ref = f32[8,192,128]{2,1,0:T(8,128)} custom-call(s32[128]{0:T(128)} %damp_ref.1, f32[1,192,128]{2,1,0:T(8,128)} %shard_map.37.packed_ref), custom_call_target="tpu_custom_call" | custom-call | tf_op jit(solution)/shard_map/pallas_call | solution.py:487
  71.6 2.5 %shard_map.39 = f32[8,192,192]{2,1,0:T(8,128)} custom-call(f32[8,192,128]{2,1,0:T(8,128)} %shard_map.38.packed_ref), custom_call_target="tpu_custom_call" | custom-call | tf_op jit(solution)/shard_map/pallas_call | solution.py:520

commit v4 on v3

--- a/solution.py
+++ b/solution.py
@@ -123,7 +123,7 @@
     barrier = pltpu.get_barrier_semaphore()
     for device in devices:
         pl.semaphore_signal(barrier, inc=1, device_id=device, device_id_type=pl.DeviceIdType.MESH)
-    pl.semaphore_wait(barrier, len(devices))
+    return functools.partial(pl.semaphore_wait, barrier, len(devices))
 
 
 RING = 4
@@ -135,7 +135,7 @@
 TAIL_US = 0.2
 HOP_US = 2.5
 LINK_RATE = 46.6e3
-VISITS = ((2, 2), (2, 1), (1, 2), (2, 3), (3, 2), (2, 0), (0, 2), (1, 0), (3, 0), (0, 0), (1, 1), (3, 3), (1, 3), (3, 1), (0, 1), (0, 3))
+VISITS = ((3, 2), (2, 2), (2, 3), (0, 2), (2, 1), (1, 2), (1, 1), (2, 0), (3, 3), (1, 3), (3, 1), (0, 3), (3, 0), (0, 1), (0, 0), (1, 0))
 
 
 def place():
@@ -258,10 +258,40 @@
                 copy.wait_send()
 
 
+class Last:
+    def __init__(self, part, acc, near, sem_near, sem_send):
+        self.part, self.level, self.acc, self.near, self.sem_near, self.sem_send = part, 2, acc, near, sem_near, sem_send
+        self.axis = ORDERS[part][2]
+        self.rows = pl.ds(part * BLK, BLK)
+        self.size = BLK * 2 * BLK * 4
+
+    def copy(self, block):
+        spot = [0, 0, 0]
+        spot[self.axis] = block
+        return remote(
+            self.acc.at[tuple(spot) + (self.rows,)],
+            self.near.at[block - 1],
+            self.sem_send.at[block - 1],
+            self.sem_near.at[block - 1],
+            neighbour(self.axis, block),
+        )
+
+    def settle(self):
+        self.acc[0, 0, 0, self.rows] += self.near[0] + self.near[1] + self.near[2]
+
+    def finish(self):
+        for block in (1, 2, 3):
+            self.copy(block).wait_send()
+
+
 def scatter_kernel(rows_ref, weights_ref, out_ref, acc, sent, got, mine, wide, columns, *rest):
     x, y, z, core = place()
     sem_in, sem_core = rest[-2:]
-    stages = [[(First(part, acc, *refs) if level == 0 else Later(part, level, acc, *refs)) for part in range(3) for refs in [rest[5 * (3 * level + part) :][:5]]] for level in range(3)]
+    stages = [
+        [First(part, acc, *rest[5 * part :][:5]) for part in range(3)],
+        [Later(part, 1, acc, *rest[15 + 5 * part :][:5]) for part in range(3)],
+        [Last(part, acc, *rest[30 + 3 * part :][:3]) for part in range(3)],
+    ]
     span = RING * HD
     partner = {"head": lax.axis_index("head") // 2 * 2 + 1 - core}
     count = len(VISITS)
@@ -279,6 +309,7 @@
         slot = v % AHEAD
         return pltpu.make_async_copy(rows_ref.at[:, pl.ds(start, span)], columns.at[slot], sem_in.at[slot])
 
+    met = greet([partner] + [to for stage in stages[0] for to in stage.to] + [neighbour(axis, 2) for axis in range(3)])
     for v in range(AHEAD):
         fetch(v).start()
     for k in range(wide.shape[0] // (2 * BLK)):
@@ -334,18 +365,14 @@
             elif group:
                 sends = [message(t.direct_copy(group // 2), t, group // 2, 2, (t, "direct", group // 2))]
             plan((s, group), [s.visit(0, slot) for slot in slots], arrivals, functools.partial(s.settle, group), sends)
-        for before, now, after in ((s, t, u), (t, u, None)):
-            for d in (0, 1):
-                sends = [message(now.near_copy(d, g), now, d, 1, (now, "near", d, g), len(now.groups())) for g in now.groups()]
-                plan((now, "relay", d), [(before, (1, 3)[d])], [(now, "far", d)], functools.partial(now.relay, d), sends)
-            for g in now.groups():
-                arrivals = [(now, kind, d, g) for d in (0, 1) for kind in ("near",)] + [(now, "direct", d) for d in (0, 1)]
-                sends = []
-                if after and g == 2:
-                    sends = [message(after.far_copy(d), after, d, 0, (after, "far", d)) for d in (0, 1)]
-                elif after and g:
-                    sends = [message(after.direct_copy(g // 2), after, g // 2, 2, (after, "direct", g // 2))]
-                plan((now, g), [(before, 0)], arrivals, functools.partial(now.settle, g), sends)
+        for d in (0, 1):
+            sends = [message(t.near_copy(d, g), t, d, 1, (t, "near", d, g), RING) for g in FAR_FIRST]
+            plan((t, "relay", d), [(s, (1, 3)[d])], [(t, "far", d)], functools.partial(t.relay, d), sends)
+        for g in FAR_FIRST:
+            arrivals = [(t, "near", d, g) for d in (0, 1)] + [(t, "direct", d) for d in (0, 1)]
+            sends = [message(u.copy(g), u, g // 3, 0, (u, g))] if g else []
+            plan((t, g), [(s, 0)], arrivals, functools.partial(t.settle, g), sends)
+        plan((u, 0), [(t, 0)], [(u, block) for block in (1, 2, 3)], u.settle, [])
 
     done, waited, due, free = set(), set(), {}, {}
     pending = list(events)
@@ -377,7 +404,7 @@
         for _, _, _, work, _ in ready:
             work()
         if r == -1:
-            greet([partner] + [to for stage in stages[0] for to in stage.to])
+            met()
         if r + 1 < count:
             exchange(r + 1).start()
         for v in now:
@@ -410,6 +437,9 @@
                 far = (2,) + tuple(RING if a in free else 1 for a in range(3)) + (HALF, lanes)
                 near = far[:-2] + (BLK, lanes)
                 sems = (2,), (2, RING + 1), (3, 2)
+                if level == 2:
+                    rings += [pltpu.VMEM((3, BLK, lanes), f32), *map(pltpu.SemaphoreType.DMA, ((3,), (3,)))]
+                    continue
             else:
                 slots, each = ((RING, RING), (RING, RING), (RING * RING, 1))[part]
                 far = (slots, each, BLK, lanes)
@@ -450,7 +480,7 @@
         rows = out_ref.at[dp, pl.ds(part * early, early)]
         return [remote(rows, rows, sems.at[0, part, o], sems.at[1, part, o], {"dp": peer}) for o, peer in enumerate(peers)]
 
-    greet([{"dp": peer} for peer in peers])
+    met = greet([{"dp": peer} for peer in peers])
     got = packed_ref[0] / total
     even = dp % 2 == 0
     a11, a22, a33, low, a32 = (jnp.where(even, a, b) for a, b in zip(unpack_even(got), unpack_odd(got)))
@@ -468,6 +498,7 @@
     w21 = -dot(w22, below[:BLK])
     out_ref[dp, :BLK] = jnp.concatenate((w11, w22), axis=1)
     out_ref[dp, BLK:early] = fold(w21)
+    met()
     for copy in share(0):
         copy.start()
     l32 = dot_t(a32 - square[BLK:, :BLK], w22)

time: 74.4 us -> 65.1 us (0.87)
  Pallas kernels: 74 us -> 64.7 us
    pallas_call x1, Pallas kernels: 53.4 us -> 44.4 us  [gram_sums(): pl.pallas_call(scatter_kernel, in_specs=[pl.BlockSpec(memory_space=pl.ANY...]
where the time goes in v4:
time: 65.1 us; the launch traced here: 64.9 us
  Pallas kernels  64.7 us (99%)
    pallas_call x1, Pallas kernels, gram_sums(): pl.pallas_call(scatter_kernel, in_specs=[pl.BlockSpec(memory_space=pl.ANY...  44.4 us
    pallas_call x1, Pallas kernels, whiten(): pl.pallas_call(functools.partial(whiten_kernel, total), in_specs=[pl.Bloc...  17.9 us
    pallas_call x1, Pallas kernels, unpack(): pl.pallas_call(unpack_kernel, in_specs=[pl.BlockSpec(memory_space=pltpu.V...  2.47 us

profile of v4, /device:TPU:0, one launch (start us, length us, event | category | flops | bytes accessed | tf_op | source)
XLA Modules:
  0.0 64.9 jit_solution(3896704457354236000)
XLA Ops:
  0.0 44.4 %shard_map.37.packed_ref = f32[1,192,128]{2,1,0:T(8,128)} custom-call(bf16[384,24576]{1,0:T(8,128)(2,1)} %rows_ref.1, s32[384]{0:T(512)} %weights_ref.1), custom_call_target="tpu_custom_call" | custom-call | tf_op jit(solution)/shard_map/pallas_call | solution.py:449
  44.4 17.9 %shard_map.38.packed_ref = f32[8,192,128]{2,1,0:T(8,128)} custom-call(s32[128]{0:T(128)} %damp_ref.1, f32[1,192,128]{2,1,0:T(8,128)} %shard_map.37.packed_ref), custom_call_target="tpu_custom_call" | custom-call | tf_op jit(solution)/shard_map/pallas_call | solution.py:518
  62.2 2.5 %shard_map.39 = f32[8,192,192]{2,1,0:T(8,128)} custom-call(f32[8,192,128]{2,1,0:T(8,128)} %shard_map.38.packed_ref), custom_call_target="tpu_custom_call" | custom-call | tf_op jit(solution)/shard_map/pallas_call | solution.py:551

commit v5 on v4

--- a/solution.py
+++ b/solution.py
@@ -14,18 +14,18 @@
 
 def store_pair(rows, wide, out, at, after):
     weighted = rows * wide
-    contract = (((0,), (0,)), ((), ()))
-    width = 4 * BLK
-    first = lax.dot_general(rows[:, :width], weighted[:, :width], contract, preferred_element_type=jnp.float32)
-    second = lax.dot_general(rows[:, -width:], weighted[:, -width:], contract, preferred_element_type=jnp.float32)
-    two = 2 * BLK
+    across = (((1,), (0,)), ((), ()))
+    width, two = 4 * BLK, 2 * BLK
+    first = lax.dot_general(rows[:, :HD], weighted[:, :width], (((0,), (0,)), ((), ())), preferred_element_type=jnp.float32)
+    turned = rows[:, -width:].T[BLK:]
+    second = lax.dot_general(turned, weighted[:, -width:], across, preferred_element_type=jnp.float32)
     lanes = lax.broadcasted_iota(jnp.int32, (BLK, two), 1)
-    corner = pltpu.roll(first[two : two + BLK, two:], BLK, 1)
+    corner = pltpu.roll(first[two:, two:], BLK, 1)
     out[at, :BLK, :] = jnp.where(lanes < BLK, first[:BLK, :two], corner)
     out[at, BLK:, :] = first[BLK:HD, :two]
-    out[after, :two, :] = second[BLK : BLK + two, two:]
-    corner = pltpu.roll(second[BLK:two, :two], BLK, 1)
-    out[after, two:, :] = jnp.where(lanes < BLK, corner, second[HD:, two:])
+    out[after, :two, :] = second[:two, two:]
+    corner = pltpu.roll(second[:BLK, :two], BLK, 1)
+    out[after, two:, :] = jnp.where(lanes < BLK, corner, second[two:, two:])
 
 
 def dot(a, b):
@@ -131,7 +131,7 @@
 FAR_FIRST = (2, 1, 3, 0)
 ORDERS = ((0, 1, 2), (1, 2, 0), (2, 0, 1))
 AHEAD = 6
-VISIT_US = 1.0
+VISIT_US = 0.85
 TAIL_US = 0.2
 HOP_US = 2.5
 LINK_RATE = 46.6e3
@@ -149,6 +149,52 @@
     spot[axis] = (spot[axis] + step) % RING
     x, y, z, core = spot
     return {"head": (x * 2 + y // 2) * 2 + core, "dp": y % 2 * RING + z}
+
+
+def fold(block):
+    return jnp.concatenate((block[:HALF], block[HALF:]), axis=1)
+
+
+def whiten(packed, damp_ref, total, out_ref, sems):
+    head, dp = lax.axis_index("head"), lax.axis_index("dp")
+    n_dp = out_ref.shape[0]
+    peers = [lax.rem(dp + o, n_dp) for o in range(1, n_dp)]
+    two, early = 2 * BLK, HD // 2
+
+    def share(part):
+        rows = out_ref.at[dp, pl.ds(part * early, early)]
+        return [remote(rows, rows, sems.at[0, part, o], sems.at[1, part, o], {"dp": peer}) for o, peer in enumerate(peers)]
+
+    got = packed / total
+    even = dp % 2 == 0
+    a11, a22, a33, low, a32 = (jnp.where(even, a, b) for a, b in zip(unpack_even(got), unpack_odd(got)))
+    diag = lax.broadcasted_iota(jnp.int32, (BLK, BLK), 0) == lax.broadcasted_iota(jnp.int32, (BLK, BLK), 1)
+    trace = jnp.sum(jnp.where(diag, a11 + a22 + a33, 0.0), axis=(0, 1), keepdims=True)
+    level = trace / HD + 1e-06
+    power = damp_ref[head * n_dp + dp]
+    damp = jnp.where(power % 2 == 1, 0.5, 1.0) * jnp.where(power >= 2, 0.25, 1.0)
+    shift = jnp.where(diag, damp * level, 0.0)
+    w11 = inverse_factor(a11 + shift)
+    l1 = dot_t(low, w11)
+    square = dot_t(l1, l1)
+    below = dot(l1, w11)
+    w22 = inverse_factor(a22 + shift - square[:BLK, :BLK])
+    w21 = -dot(w22, below[:BLK])
+    out_ref[dp, :BLK] = jnp.concatenate((w11, w22), axis=1)
+    out_ref[dp, BLK:early] = fold(w21)
+    for copy in share(0):
+        copy.start()
+    l32 = dot_t(a32 - square[BLK:, :BLK], w22)
+    w33 = inverse_factor(a33 + shift - square[BLK:, BLK:] - dot_t(l32, l32))
+    w31 = -dot(w33, below[BLK:] + dot(l32, w21))
+    w32 = -dot(w33, dot(l32, w22))
+    out_ref[dp, early:two] = fold(w33)
+    out_ref[dp, two:] = jnp.concatenate((w31, w32), axis=1)
+    for copy in share(1):
+        copy.start()
+    for part in (0, 1):
+        for copy in share(part):
+            copy.wait()
 
 
 class First:
@@ -284,9 +330,9 @@
             self.copy(block).wait_send()
 
 
-def scatter_kernel(rows_ref, weights_ref, out_ref, acc, sent, got, mine, wide, columns, *rest):
+def factor_kernel(total, rows_ref, weights_ref, damp_ref, out_ref, acc, sent, got, mine, wide, columns, *rest):
     x, y, z, core = place()
-    sem_in, sem_core = rest[-2:]
+    sem_in, sem_core, sem_share = rest[-3:]
     stages = [
         [First(part, acc, *rest[5 * part :][:5]) for part in range(3)],
         [Later(part, 1, acc, *rest[15 + 5 * part :][:5]) for part in range(3)],
@@ -309,7 +355,9 @@
         slot = v % AHEAD
         return pltpu.make_async_copy(rows_ref.at[:, pl.ds(start, span)], columns.at[slot], sem_in.at[slot])
 
-    met = greet([partner] + [to for stage in stages[0] for to in stage.to] + [neighbour(axis, 2) for axis in range(3)])
+    n_dp = out_ref.shape[0]
+    peers = [{"dp": lax.rem(lax.axis_index("dp") + o, n_dp)} for o in range(1, n_dp)]
+    met = greet([partner] + [to for stage in stages[0] for to in stage.to] + [neighbour(axis, 2) for axis in range(3)] + peers)
     for v in range(AHEAD):
         fetch(v).start()
     for k in range(wide.shape[0] // (2 * BLK)):
@@ -417,7 +465,7 @@
             free[link] = max(free.get(link, 0.0), clock) + size / LINK_RATE + 0.08
             due[m] = free[link] + HOP_US
         r += 1
-    out_ref[0] = acc[0, 0, 0]
+    whiten(acc[0, 0, 0], damp_ref, total, out_ref, sem_share)
     for i in range(count):
         exchange(i).wait_send()
     for level in stages:
@@ -425,7 +473,7 @@
             stage.finish()
 
 
-def gram_sums(projected, weights):
+def factors(projected, weights, damp_exp, total, n_dp):
     tokens, width = projected.shape
     rows, lanes = HD, 2 * BLK
     f32 = jnp.float32
@@ -447,10 +495,14 @@
                 sems = (slots,), (2, slots), (3,)
             rings += [pltpu.VMEM(far, f32), pltpu.VMEM(near, f32), *map(pltpu.SemaphoreType.DMA, sems)]
     return pl.pallas_call(
-        scatter_kernel,
-        in_specs=[pl.BlockSpec(memory_space=pl.ANY), pl.BlockSpec(memory_space=pltpu.VMEM)],
+        functools.partial(factor_kernel, total),
+        in_specs=[
+            pl.BlockSpec(memory_space=pl.ANY),
+            pl.BlockSpec(memory_space=pltpu.VMEM),
+            pl.BlockSpec(memory_space=pltpu.SMEM),
+        ],
         out_specs=pl.BlockSpec(memory_space=pltpu.VMEM),
-        out_shape=jax.ShapeDtypeStruct((1, rows, lanes), f32),
+        out_shape=jax.ShapeDtypeStruct((n_dp, rows, lanes), f32),
         scratch_shapes=[
             pltpu.VMEM((RING, RING, RING, rows, lanes), f32),
             pltpu.VMEM((len(VISITS), RING, rows, lanes), f32),
@@ -461,68 +513,10 @@
             *rings,
             pltpu.SemaphoreType.DMA((AHEAD,)),
             pltpu.SemaphoreType.DMA((2, len(VISITS))),
+            pltpu.SemaphoreType.DMA((2, 2, n_dp - 1)),
         ],
         compiler_params=pltpu.CompilerParams(collective_id=0, has_side_effects=True, vmem_limit_bytes=60 << 20),
-    )(projected, weights)
-
-
-def fold(block):
-    return jnp.concatenate((block[:HALF], block[HALF:]), axis=1)
-
-
-def whiten_kernel(total, damp_ref, packed_ref, out_ref, sems):
-    head, dp = lax.axis_index("head"), lax.axis_index("dp")
-    n_dp = out_ref.shape[0]
-    peers = [lax.rem(dp + o, n_dp) for o in range(1, n_dp)]
-    two, early = 2 * BLK, HD // 2
-
-    def share(part):
-        rows = out_ref.at[dp, pl.ds(part * early, early)]
-        return [remote(rows, rows, sems.at[0, part, o], sems.at[1, part, o], {"dp": peer}) for o, peer in enumerate(peers)]
-
-    met = greet([{"dp": peer} for peer in peers])
-    got = packed_ref[0] / total
-    even = dp % 2 == 0
-    a11, a22, a33, low, a32 = (jnp.where(even, a, b) for a, b in zip(unpack_even(got), unpack_odd(got)))
-    diag = lax.broadcasted_iota(jnp.int32, (BLK, BLK), 0) == lax.broadcasted_iota(jnp.int32, (BLK, BLK), 1)
-    trace = jnp.sum(jnp.where(diag, a11 + a22 + a33, 0.0), axis=(0, 1), keepdims=True)
-    level = trace / HD + 1e-06
-    power = damp_ref[head * n_dp + dp]
-    damp = jnp.where(power % 2 == 1, 0.5, 1.0) * jnp.where(power >= 2, 0.25, 1.0)
-    shift = jnp.where(diag, damp * level, 0.0)
-    w11 = inverse_factor(a11 + shift)
-    l1 = dot_t(low, w11)
-    square = dot_t(l1, l1)
-    below = dot(l1, w11)
-    w22 = inverse_factor(a22 + shift - square[:BLK, :BLK])
-    w21 = -dot(w22, below[:BLK])
-    out_ref[dp, :BLK] = jnp.concatenate((w11, w22), axis=1)
-    out_ref[dp, BLK:early] = fold(w21)
-    met()
-    for copy in share(0):
-        copy.start()
-    l32 = dot_t(a32 - square[BLK:, :BLK], w22)
-    w33 = inverse_factor(a33 + shift - square[BLK:, BLK:] - dot_t(l32, l32))
-    w31 = -dot(w33, below[BLK:] + dot(l32, w21))
-    w32 = -dot(w33, dot(l32, w22))
-    out_ref[dp, early:two] = fold(w33)
-    out_ref[dp, two:] = jnp.concatenate((w31, w32), axis=1)
-    for copy in share(1):
-        copy.start()
-    for part in (0, 1):
-        for copy in share(part):
-            copy.wait()
-
-
-def whiten(packed, damp_exp, total, n_dp):
-    return pl.pallas_call(
-        functools.partial(whiten_kernel, total),
-        in_specs=[pl.BlockSpec(memory_space=pltpu.SMEM), pl.BlockSpec(memory_space=pltpu.VMEM)],
-        out_specs=pl.BlockSpec(memory_space=pltpu.VMEM),
-        out_shape=jax.ShapeDtypeStruct((n_dp,) + packed.shape[1:], jnp.float32),
-        scratch_shapes=[pltpu.SemaphoreType.DMA((2, 2, n_dp - 1))],
-        compiler_params=pltpu.CompilerParams(collective_id=1, has_side_effects=True),
-    )(damp_exp, packed)
+    )(projected, weights, damp_exp)
 
 
 def unpack_kernel(packed_ref, out_ref, whole, sems):
@@ -560,8 +554,7 @@
 def on_device(projected, weight_exp, damp_exp):
     n_dp = lax.axis_size("dp")
     total = projected.shape[0] * lax.axis_size("head") * n_dp
-    owned = gram_sums(projected, weight_exp)
-    return unpack(whiten(owned, damp_exp, float(total), n_dp))
+    return unpack(factors(projected, weight_exp, damp_exp, float(total), n_dp))
 
 
 def solution(mesh):

time: 65.1 us -> 62.7 us (0.963)
  Pallas kernels: 64.7 us -> 62.4 us
    pallas_call x2 -> x1, Pallas kernels: 62.2 us -> 59.9 us  [factors(): pl.pallas_call(functools.partial(factor_kernel, total), in_specs=[pl.Bloc...]
where the time goes in v5:
time: 62.7 us; the launch traced here: 62.5 us
  Pallas kernels  62.4 us (100%)
    pallas_call x1, Pallas kernels, factors(): pl.pallas_call(functools.partial(factor_kernel, total), in_specs=[pl.Bloc...  59.9 us
    pallas_call x1, Pallas kernels, unpack(): pl.pallas_call(unpack_kernel, in_specs=[pl.BlockSpec(memory_space=pltpu.V...  2.47 us

profile of v5, /device:TPU:0, one launch (start us, length us, event | category | flops | bytes accessed | tf_op | source)
XLA Modules:
  0.0 62.5 jit_solution(9562936061571300)
XLA Ops:
  0.0 59.9 %shard_map.37.packed_ref = f32[8,192,128]{2,1,0:T(8,128)} custom-call(bf16[384,24576]{1,0:T(8,128)(2,1)} %rows_ref.1, s32[384]{0:T(512)} %weights_ref.1, s32[128]{0:T(128)} %damp_ref.1), custom_call_target="tpu_custom_call" | custom-call | tf_op jit(solution)/shard_map/pallas_call | solution.py:497
  59.9 2.5 %shard_map.38 = f32[8,192,192]{2,1,0:T(8,128)} custom-call(f32[8,192,128]{2,1,0:T(8,128)} %shard_map.37.packed_ref), custom_call_target="tpu_custom_call" | custom-call | tf_op jit(solution)/shard_map/pallas_call | solution.py:545

commit v6 on v5

--- a/solution.py
+++ b/solution.py
@@ -133,7 +133,7 @@
 AHEAD = 6
 VISIT_US = 0.85
 TAIL_US = 0.2
-HOP_US = 2.5
+HOP_US = 3.5
 LINK_RATE = 46.6e3
 VISITS = ((3, 2), (2, 2), (2, 3), (0, 2), (2, 1), (1, 2), (1, 1), (2, 0), (3, 3), (1, 3), (3, 1), (0, 3), (3, 0), (0, 1), (0, 0), (1, 0))
 

time: 62.7 us -> 67.4 us (1.075); the launches traced: 62.5 us -> 66.4 us
  Pallas kernels: 62.4 us -> 66.2 us
    pallas_call x1, Pallas kernels: 59.9 us -> 63.7 us  [factors(): pl.pallas_call(functools.partial(factor_kernel, total), in_specs=[pl.Bloc...]
where the time goes in v6:
time: 67.4 us; the launch traced here: 66.4 us
  Pallas kernels  66.2 us (98%)
    pallas_call x1, Pallas kernels, factors(): pl.pallas_call(functools.partial(factor_kernel, total), in_specs=[pl.Bloc...  63.7 us
    pallas_call x1, Pallas kernels, unpack(): pl.pallas_call(unpack_kernel, in_specs=[pl.BlockSpec(memory_space=pltpu.V...  2.47 us

profile of v6, /device:TPU:0, one launch (start us, length us, event | category | flops | bytes accessed | tf_op | source)
XLA Modules:
  0.0 66.4 jit_solution(10230375231006457396)
XLA Ops:
  0.0 63.7 %shard_map.37.packed_ref = f32[8,192,128]{2,1,0:T(8,128)} custom-call(bf16[384,24576]{1,0:T(8,128)(2,1)} %rows_ref.1, s32[384]{0:T(512)} %weights_ref.1, s32[128]{0:T(128)} %damp_ref.1), custom_call_target="tpu_custom_call" | custom-call | tf_op jit(solution)/shard_map/pallas_call | solution.py:497
  63.7 2.5 %shard_map.38 = f32[8,192,192]{2,1,0:T(8,128)} custom-call(f32[8,192,128]{2,1,0:T(8,128)} %shard_map.37.packed_ref), custom_call_target="tpu_custom_call" | custom-call | tf_op jit(solution)/shard_map/pallas_call | solution.py:545
